TPU v7x, 32 devices: a 4x4x1 block of a 4x4x8 slice. The times are simulated.
32 devices in a mesh: dp: 1 (over z), tp: 4 (over y), cp: 8 (over x, core).
Axes of the slice: x: 4, y: 4, z: 1, core: 2. Of those that a mesh axis runs over, the one named last changes fastest.
The devices are a block of a 4x4x8 slice.
Arguments:
- hidden: bfloat16 [6, 2048, 6144], P('dp', 'cp')
- positions: int32 [6, 2048], P('dp', 'cp')
- w_dq: bfloat16 [6144, 1536], replicated
- g_q: float32 [1536], replicated
- w_uq: bfloat16 [1536, 12288], P(None, 'tp')
- w_dkv: bfloat16 [6144, 576], replicated
- g_kv: float32 [512], replicated
- w_uk: bfloat16 [512, 8192], P(None, 'tp')
- w_uv: bfloat16 [512, 8192], P(None, 'tp')
- w_o: bfloat16 [8192, 6144], P('tp')
Outputs:
- output 1: bfloat16 [6, 2048, 6144], P('dp', 'cp')
- output 2: bfloat16 [6, 2048, 512], P('dp', 'cp')
- output 3: bfloat16 [6, 2048, 64], P('dp', 'cp')
All inputs are finite; a program needn't handle non-finite values.
Results may differ from a plain program's by a relative error of at most 0.00745629.
Values are sent between devices in bfloat16 or wider.
A program may use at most 768 MiB of HBM per device.

v0:
```python
import jax
import jax.numpy as jnp
from jax import lax
from jax.sharding import PartitionSpec as P

ROPE_BASE = 10000.0
NORM_EPS = 1e-6


def rms_norm(tensor, norm_gain):
    tensor_f32 = tensor.astype(jnp.float32)
    inv_rms = lax.rsqrt(jnp.mean(tensor_f32 * tensor_f32, axis=-1, keepdims=True) + NORM_EPS)
    return (tensor_f32 * inv_rms * norm_gain).astype(jnp.bfloat16)


def rope_tables(positions, rope_dim):
    inv_freq = ROPE_BASE ** (-2.0 * jnp.arange(rope_dim // 2, dtype=jnp.float32) / rope_dim)
    angles = positions.astype(jnp.float32)[..., None] * inv_freq
    return jnp.cos(angles), jnp.sin(angles)


def rotate(tensor, cos_t, sin_t):
    tensor_f32 = tensor.astype(jnp.float32)
    half_dim = tensor_f32.shape[-1] // 2
    lower_half = tensor_f32[..., :half_dim]
    upper_half = tensor_f32[..., half_dim:]
    return jnp.concatenate([lower_half * cos_t - upper_half * sin_t,
                            lower_half * sin_t + upper_half * cos_t], axis=-1).astype(jnp.bfloat16)


def attend(q_nope, q_rope, pos_q, k_nope, k_rope, values, pos_k, soft_scale):
    scores = (jnp.einsum('nshd,nthd->nhst', q_nope, k_nope, preferred_element_type=jnp.float32)
              + jnp.einsum('nshd,ntd->nhst', q_rope, k_rope, preferred_element_type=jnp.float32)) * soft_scale
    allowed = pos_k[:, None, None, :] <= pos_q[:, None, :, None]
    scores = jnp.where(allowed, scores, -jnp.inf)
    probs_bf = jax.nn.softmax(scores, axis=-1).astype(jnp.bfloat16)
    attn_heads = jnp.einsum('nhst,nthd->nshd', probs_bf, values,
                            preferred_element_type=jnp.float32).astype(jnp.bfloat16)
    return attn_heads.reshape(attn_heads.shape[0], attn_heads.shape[1], -1)


def solution(mesh):
    def local_step(x_blk, pos_blk, w_dq, g_q, w_uq, w_dkv, g_kv, w_uk, w_uv, w_o):
        num_seq = x_blk.shape[0]
        seq_dev = x_blk.shape[1]
        kv_rank = g_kv.shape[0]
        rope_dim = w_dkv.shape[1] - kv_rank
        heads_dev = (w_uq.shape[1] - w_uk.shape[1]) // rope_dim
        nope_dim = w_uk.shape[1] // heads_dev
        v_dim = w_uv.shape[1] // heads_dev
        soft_scale = (nope_dim + rope_dim) ** -0.5
        cos_t, sin_t = rope_tables(pos_blk, rope_dim)
        q_latent = jnp.einsum('nsd,dr->nsr', x_blk, w_dq, preferred_element_type=jnp.float32).astype(jnp.bfloat16)
        q_full = jnp.einsum('nsr,rk->nsk', rms_norm(q_latent, g_q), w_uq,
                            preferred_element_type=jnp.float32).astype(jnp.bfloat16)
        q_full = q_full.reshape(num_seq, seq_dev, heads_dev, nope_dim + rope_dim)
        q_nope = q_full[..., :nope_dim]
        q_rope = rotate(q_full[..., nope_dim:], cos_t[:, :, None, :], sin_t[:, :, None, :])
        kv_joint = jnp.einsum('nsd,dc->nsc', x_blk, w_dkv, preferred_element_type=jnp.float32).astype(jnp.bfloat16)
        latent = rms_norm(kv_joint[..., :kv_rank], g_kv)
        k_rope = rotate(kv_joint[..., kv_rank:], cos_t, sin_t)
        k_nope = jnp.einsum('nsc,ck->nsk', latent, w_uk, preferred_element_type=jnp.float32).astype(jnp.bfloat16)
        k_nope = k_nope.reshape(num_seq, seq_dev, heads_dev, nope_dim)
        values = jnp.einsum('nsc,ck->nsk', latent, w_uv, preferred_element_type=jnp.float32).astype(jnp.bfloat16)
        values = values.reshape(num_seq, seq_dev, heads_dev, v_dim)
        k_nope_all = lax.all_gather(k_nope, 'cp', axis=1, tiled=True)
        values_all = lax.all_gather(values, 'cp', axis=1, tiled=True)
        k_rope_all = lax.all_gather(k_rope, 'cp', axis=1, tiled=True)
        pos_all = lax.all_gather(pos_blk, 'cp', axis=1, tiled=True)
        attn_out = attend(q_nope, q_rope, pos_blk, k_nope_all, k_rope_all, values_all, pos_all, soft_scale)
        part_out = jnp.einsum('nsk,kd->nsd', attn_out, w_o, preferred_element_type=jnp.float32)
        head_sum = lax.psum(part_out, 'tp')
        out_hidden = (x_blk.astype(jnp.float32) + head_sum).astype(jnp.bfloat16)
        return out_hidden, latent, k_rope

    seq_spec = P('dp', 'cp', None)
    in_specs = (seq_spec, P('dp', 'cp'), P(None, None), P(None), P(None, 'tp'), P(None, None), P(None),
                P(None, 'tp'), P(None, 'tp'), P('tp', None))
    return jax.shard_map(local_step, mesh=mesh, in_specs=in_specs,
                         out_specs=(seq_spec, seq_spec, seq_spec), check_vma=False)
```

profile of v0, /device:TPU:97, one launch (start us, length us, event | category | flops | bytes accessed | tf_op | source)
XLA Modules:
  0.0 1305.8 jit_solution(13348805702504552197)
XLA Ops:
  7.2 0.0 copy-start
  7.2 0.1 all-gather.8.cloned.1.call-start
  7.3 0.0 copy-start.6
  7.3 0.0 copy-start.7
  7.3 17.2 %fusion.40 = bf16[6,256,576]{1,2,0:T(8,128)(2,1)S(1)} fusion(bf16[6,256,6144]{2,1,0:T(8,128)(2,1)} %param.10, bf16[6144,576]{0,1:T(8,128)(2,1)} %param.15), kind=kOutput, calls=%fused_computation.47 | convolution fusion | flops 10872520704 | bytes 27721728 | tf_op jit(solution)/shard_map/nsd,dc->nsc/dot_general | solution.py:59
  24.5 0.0 copy-start.2
  24.5 1.2 copy-done.2
  25.8 0.0 copy-done.6
  25.8 0.8 subtract_convert_fusion.1
  26.6 0.7 pad_maximum_fusion
  27.3 0.1 all-gather.8.cloned.1.call-update
  27.3 0.1 all-gather.6.cloned.1.call-start
  27.4 1.7 fusion.31
  29.2 0.0 copy-done.7
  29.2 1.8 fusion.33
  31.0 0.0 copy-done
  31.0 0.0 copy-start.3
  31.0 3.7 convert_bitcast_fusion
  34.7 0.0 copy-done.3
  34.7 4.4 copy.40
  39.2 0.0 copy-start.4
  39.2 0.1 all-gather.6.cloned.1.call-update
  39.2 0.1 all-gather.4.cloned.1.call-start
  39.3 1.3 copy-done.4
  40.6 7.0 convolution_convert_fusion
  47.5 8.6 copy.36
  56.1 0.1 all-gather.4.cloned.1.call-update
  56.2 0.0 copy-start.8
  56.2 0.2 all-reduce.2.cloned.1.call-start
  56.5 38.0 %fusion.8 = (f32[6,256]{1,0:T(8,128)S(1)}, bf16[6,256,1536]{2,1,0:T(8,128)(2,1)S(1)}) fusion(bf16[6,256,6144]{2,1,0:T(8,128)(2,1)} %param.10, bf16[6144,1536]{1,0:T(8,128)(2,1)} %param.12), kind=kOutput, calls=%fused_computation.14 | convolution fusion | flops 29000464384 | bytes 42473472 | tf_op jit(solution)/shard_map/nsd,dr->nsr/dot_general | solution.py:53
  94.5 0.0 copy-done.8
  94.5 19.5 %fusion.15 = bf16[6,256,3072]{2,1,0:T(8,128)(2,1)} fusion(bf16[1536,3072]{1,0:T(8,128)(2,1)} %param.14, bf16[6,256,1536]{2,1,0:T(8,128)(2,1)S(1)} %get-tuple-element.16, f32[1536]{0:T(1024)S(1)} %copy-done.8, f32[6,256]{1,0:T(8,128)S(1)} %add_rsqrt_fusion), kind=kOutput, calls=%fused_computation.21 | convolution fusion | flops 14509670400 | bytes 23605248 | tf_op jit(solution)/shard_map/nsr,rk->nsk/dot_general | solution.py:54
  113.9 12.6 copy.24
  126.6 21.9 %all_gather.13 = s32[6,2048]{1,0:T(8,128)S(1)} all-gather(s32[6,256]{1,0:T(8,128)S(1)} %copy-done.6), channel_id=1, replica_groups=mesh['dp'=1,'tp'=4,'cp'=8] {'cp'}, dimensions={1}, use_global_device_ids=true | all-gather | bytes 55296 | tf_op jit(solution)/shard_map/all_gather | solution.py:69
  148.4 2.8 slice_convert_fusion
  151.2 2.9 subtract_convert_fusion
  154.1 2.0 broadcast_compare_fusion
  156.1 0.0 all-gather.8.cloned.1.call-done
  156.1 67.5 %fusion.34 = f32[6,2048,256,16]{1,2,3,0:T(8,128)} fusion(bf16[6,256,16,32]{1,3,2,0:T(8,128)(2,1)} %get-tuple-element.10, bf16[6,256,16,32]{1,3,2,0:T(8,128)(2,1)} %get-tuple-element.9, bf16[6,2048,64]{1,2,0:T(8,128)(2,1)} %all-gather.8.cloned.1.call-done), kind=kOutput, calls=%fused_computation.39 | convolution fusion | flops 6448742400 | bytes 206045184 | tf_op jit(solution)/shard_map/nshd,ntd->nhst/dot_general | solution.py:33
  223.6 58.9 %all-gather.6.cloned.1.call-done = bf16[6,2048,16,128]{3,1,2,0:T(8,128)(2,1)} async-done(((bf16[6,256,16,128]{3,1,2,0:T(8,128)(2,1)}), bf16[6,2048,16,128]{3,1,2,0:T(8,128)(2,1)}) %all-gather.6.cloned.1.call-update) | async-done | bytes 50331664 | tf_op jit(solution)/shard_map/all_gather | solution.py:66
  282.5 160.9 %fusion.47 = (f32[6,16,256]{2,1,0:T(8,128)S(1)}, f32[6,16,256,2048]{3,2,1,0:T(8,128)}) fusion(f32[6,2048,256,16]{1,2,3,0:T(8,128)} %fusion.34, bf16[6,2048,16,128]{3,1,2,0:T(8,128)(2,1)} %all-gather.6.cloned.1.call-done, pred[6,256,2048]{2,1,0:T(8,128)(4,1)S(1)} %broadcast_compare_fusion, bf16[6,256,16,192]{1,3,2,0:T(8,128)(2,1)} %bitcast.63), kind=kOutput, calls=%fused_computation.61 | convolution fusion | flops 13136562176 | bytes 462520320 | tf_op jit(solution)/shard_map/sub | solution.py:36
  443.5 74.8 %all-gather.4.cloned.1.call-done = bf16[6,2048,16,128]{1,3,2,0:T(8,128)(2,1)} async-done(((bf16[6,256,16,128]{1,3,2,0:T(8,128)(2,1)}), bf16[6,2048,16,128]{1,3,2,0:T(8,128)(2,1)}) %all-gather.4.cloned.1.call-update) | async-done | bytes 50331664 | tf_op jit(solution)/shard_map/all_gather | solution.py:67
  518.3 78.8 %fusion.30 = bf16[6,16,128,256]{3,2,1,0:T(8,128)(2,1)} fusion(bf16[6,2048,16,128]{1,3,2,0:T(8,128)(2,1)} %all-gather.4.cloned.1.call-done, f32[6,16,256,2048]{3,2,1,0:T(8,128)} %get-tuple-element.18, f32[6,16,256]{2,1,0:T(8,128)S(1)} %get-tuple-element.17), kind=kOutput, calls=%fused_computation.34 | convolution fusion | flops 12988710912 | bytes 258048000 | tf_op jit(solution)/shard_map/nhst,nthd->nshd/dot_general | solution.py:37
  597.0 47.6 %fusion.4 = f32[6,256,6144]{2,1,0:T(8,128)} fusion(bf16[6,256,2048]{1,2,0:T(8,128)(2,1)} %bitcast.66, bf16[2048,6144]{1,0:T(8,128)(2,1)} %param.19), kind=kOutput, calls=%fused_computation.8 | convolution fusion | flops 38654705664 | bytes 69206016 | tf_op jit(solution)/shard_map/nsk,kd->nsd/dot_general | solution.py:71
  644.7 0.0 copy-start.5
  644.7 0.1 all-reduce.2.cloned.1.call-update
  644.7 1.3 copy-done.5
  646.1 1.6 copy.30
  647.6 625.4 %all-reduce.2.cloned.1.call-done = f32[6,256,6144]{2,1,0:T(8,128)} async-done(((f32[6,256,6144]{2,1,0:T(8,128)}), f32[6,256,6144]{2,1,0:T(8,128)}) %all-reduce.2.cloned.1.call-update) | async-done | bytes 37748752 | tf_op jit(solution)/shard_map/psum | solution.py:72
  1273.1 0.0 copy-start.1
  1273.1 25.7 %add_convert_fusion = bf16[6,256,6144]{2,1,0:T(8,128)(2,1)} fusion(f32[6,256,6144]{2,1,0:T(8,128)} %all-reduce.2.cloned.1.call-done, bf16[6,256,6144]{2,1,0:T(8,128)(2,1)} %param.10), kind=kLoop, calls=%fused_computation.7 | loop fusion | flops 28311552 | bytes 75497472 | tf_op jit(solution)/shard_map/convert_element_type | solution.py:73
  1298.8 0.0 copy-done.1
  (5 shorter events, 0.1 us)
Async XLA Ops:
  7.2 23.8 %copy-start = (bf16[512,2048]{1,0:T(8,128)(2,1)S(1)}, bf16[512,2048]{1,0:T(8,128)(2,1)}, u32[]{:S(2)}) copy-start(bf16[512,2048]{1,0:T(8,128)(2,1)} %param.17) | copy-start | bytes 6291460
  7.2 148.9 %all-gather.8.cloned.1.call-start = ((), (), s32[]{:S(2)}) async-start(), calls=%async_computation.2 | async-start | bytes 1769472 | tf_op jit(solution)/shard_map/all_gather | solution.py:68
  7.3 18.5 %copy-start.6 = (s32[6,256]{1,0:T(8,128)S(1)}, s32[6,256]{1,0:T(8,128)}, u32[]{:S(2)}) copy-start(s32[6,256]{1,0:T(8,128)} %param.11) | copy-start | bytes 18436
  7.3 21.9 %copy-start.7 = (f32[512]{0:T(512)S(1)}, f32[512]{0:T(512)}, u32[]{:S(2)}) copy-start(f32[512]{0:T(512)} %param.16) | copy-start | bytes 6148
  24.5 1.2 copy-start.2
  27.3 255.2 %all-gather.6.cloned.1.call-start = ((), (), s32[]{:S(2)}) async-start(), calls=%async_computation.1 | async-start | bytes 56623104 | tf_op jit(solution)/shard_map/all_gather | solution.py:66
  31.0 3.7 copy-start.3
  39.2 1.4 copy-start.4
  39.2 479.0 %all-gather.4.cloned.1.call-start = ((), (), s32[]{:S(2)}) async-start(), calls=%async_computation | async-start | bytes 56623104 | tf_op jit(solution)/shard_map/all_gather | solution.py:67
  56.2 38.3 %copy-start.8 = (f32[1536]{0:T(1024)S(1)}, f32[1536]{0:T(1024)}, u32[]{:S(2)}) copy-start(f32[1536]{0:T(1024)} %param.13) | copy-start | bytes 18436
  56.2 1216.9 %all-reduce.2.cloned.1.call-start = ((), (), s32[]{:S(2)}) async-start(), calls=%async_computation.3 | async-start | bytes 75497472 | tf_op jit(solution)/shard_map/psum | solution.py:72
  644.7 1.4 copy-start.5
  1273.1 25.7 %copy-start.1 = (bf16[512,2048]{1,0:T(8,128)(2,1)S(1)}, bf16[512,2048]{1,0:T(8,128)(2,1)}, u32[]{:S(2)}) copy-start(bf16[512,2048]{1,0:T(8,128)(2,1)} %param.17) | copy-start | bytes 6291460
Sparse Core Ops, SparseCore 0:
  27.5 26.3 all-gather.7
  55.5 227.0 all-gather.5
  284.1 234.0 all-gather.3
  644.9 628.1 all-reduce.1
where the time goes:
time: 1310 us
  waiting for transfers between devices  759 us (58%)
  matrix products  440 us (34%)
  other arithmetic  38.4 us (3%)
  local copies, waits for them, and re-layouts  31.1 us (2%)
  blocking collectives  21.9 us (2%)
  between operations  14.4 us (1%)
    psum x1, waiting for transfers between devices, local_step(): head_sum = lax.psum(part_out, 'tp')  625 us
    sub x1, matrix products, attend(): probs_bf = jax.nn.softmax(scores, axis=-1).astype(jnp.bfloat16)  161 us
    dot_general x1, matrix products, attend(): jnp.einsum('nhst,nthd->nshd', probs_bf, values, preferred_element_type=jn...  78.8 us
    all_gather x1, waiting for transfers between devices, local_step(): values_all = lax.all_gather(values, 'cp', axis=1, tiled=True)  74.8 us
    dot_general x1, matrix products, attend(): jnp.einsum('nshd,ntd->nhst', q_rope, k_rope, preferred_element_type=jnp.f...  67.5 us
    all_gather x1, waiting for transfers between devices, local_step(): k_nope_all = lax.all_gather(k_nope, 'cp', axis=1, tiled=True)  58.9 us
    dot_general x1, matrix products, local_step(): jnp.einsum('nsk,kd->nsd', attn_out, w_o, preferred_element_type=jnp.float32)  47.6 us
    dot_general x1, matrix products, local_step(): jnp.einsum('nsd,dr->nsr', x_blk, w_dq, preferred_element_type=jnp.float32)  38 us
  transfers between devices with their start and end apart: 4, of which 3 were waited for; matrix products, arithmetic and copies ran while one was open for 26% of the time, Pallas kernels for 0%

commit v1 on v0

v1 whole, which is shorter than its diff:
```python
import functools
import jax, jax.numpy as jnp
from jax import lax
from jax.experimental import pallas as pl
from jax.experimental.pallas import tpu as pltpu
from jax.sharding import PartitionSpec as P

F32, BF16 = jnp.float32, jnp.bfloat16
NEG = float("-inf")
LOG2E = 1.4426950408889634
LANES, HALF, MXU, TRIG = 128, 64, 256, 384
HALVES = 2
SOURCES = 4


MESH = pl.DeviceIdType.MESH
NORM_EPS = 1e-6


class Place:
    def __init__(self, n_tp, n_cp):
        self.dp, self.y, self.c = (lax.axis_index(a) for a in ("dp", "tp", "cp"))
        y, c = self.y, self.c
        self.n_tp = n_tp
        self.core = lax.rem(c, HALVES)
        self.partner = c + 1 - HALVES * self.core
        self.right, self.left, self.far = (lax.rem(c + k, n_cp) for k in (2, n_cp - 2, n_cp // HALVES))
        self.up, self.dn, self.dg = (lax.rem(y + k, n_tp) for k in (1, n_tp - 1, n_tp // HALVES))
        self.flip = lax.rem(y + self.core, HALVES)
        self.mate = lax.rem(y + 1 + HALVES * self.flip, n_tp)
        self.other = lax.rem(y + 3 - HALVES * self.flip, n_tp)

    def block(self, row, core):
        return lax.div(lax.rem(row + (self.n_tp - 1) * core, self.n_tp), HALVES)

    def greet(self, peers):
        barrier = pltpu.get_barrier_semaphore()
        for yy, cc in peers:
            pl.semaphore_signal(barrier, inc=1, device_id=(self.dp, yy, cc), device_id_type=MESH)
        pl.semaphore_wait(barrier, len(peers))

    def copy(self, src, dst, ss, rs, yy, cc):
        return pltpu.make_async_remote_copy(src_ref=src, dst_ref=dst, send_sem=ss, recv_sem=rs,
                                            device_id=(self.dp, yy, cc), device_id_type=MESH)

    def o_sends(self, own, par, dst, ss, rs):
        tb, tp = self.block(self.y, self.core), self.block(self.y, 1 - self.core)
        ways = [(own, tb, 1, 0, self.mate, self.c), (own, 1 - tb, 2, 0, self.other, self.c), (par, tp, 0, 1, self.y, self.partner),
                (par, tp, 1, 1, self.other, self.partner), (par, 1 - tp, 2, 1, self.mate, self.partner)]
        return [self.copy(a.at[blk], dst(src, part), ss.at[k], rs.at[k], yy, cc)
                for k, (a, blk, src, part, yy, cc) in enumerate(ways)]

    def o_forwards(self, src, dst, ss, rs):
        return [self.copy(src(2, part), dst(3, part), ss.at[5 + part], rs.at[5 + part], self.mate, self.c) for part in range(HALVES)]


def attn_kernel(dims, tab, *refs):
    G, NB, BL, HP, scale2, n_tp, n_cp = dims
    CK = HALVES * BL
    H = HALVES * HP
    q_own, q_par, cs_own, cs_par, wkT, wv, lat, wf = refs[:8]
    ost_own, ost_par, obuf, wx = refs[8:12]
    latbuf, KT, V, Q, sF, sS, mx, lsum, acc, ob, sem, osem, oss, ors, wss, wrs = refs[12:]
    n = pl.program_id(0)
    me = Place(n_tp, n_cp)
    rows_ = ((me.up, me.c), (me.dn, me.c), (me.up, me.partner), (me.dn, me.partner))
    w_to = ((me.y, me.partner), (me.y, me.right), (me.y, me.left))

    def w_send(k, slot):
        return me.copy(wf, wx.at[slot], wss.at[k], wrs.at[k], *w_to[k])

    def copies(i):
        return [pltpu.make_async_copy(lat.at[p, i], latbuf.at[pl.ds(HALVES * p, HALVES)], sem.at[p]) for p in range(n_cp)]

    def o_store(i):
        return [pltpu.make_async_copy(ob.at[k], dst.at[i], osem.at[k]) for k, dst in enumerate((ost_own, ost_par))]

    def o_sends(i):
        return me.o_sends(ost_own.at[i], ost_par.at[i], lambda s, p: obuf.at[s, p, i], oss.at[i], ors.at[i])

    def o_forwards(i):
        at = lambda s, p: obuf.at[s, p, i]
        return me.o_forwards(at, at, oss.at[i], ors.at[i])

    @pl.when(n == 0)
    def _():
        for c in copies(0):
            c.start()
        me.greet(rows_ + w_to)
        for k in range(3):
            w_send(k, me.c).start()

    @pl.when(n > 0)
    def _():
        for c in o_store(n - 1):
            c.wait()
        for s in o_sends(n - 1):
            s.start()

    lane = lax.broadcasted_iota(jnp.int32, (BL, LANES), 1)
    low64 = lane < HALF
    low32 = lax.rem(lane, HALF) < 32
    for src_i, (q, cs) in enumerate(((q_own, cs_own), (q_par, cs_par))):
        for half in range(HALVES):
            r0 = (half * 2 + src_i) * BL
            rows = pl.ds(half * BL, BL)
            ct = cs[rows, :LANES]
            st = cs[rows, LANES:MXU]
            for p in range(HP):
                a = q[0, rows, p * TRIG:p * TRIG + LANES]
                b = q[0, rows, p * TRIG + LANES:p * TRIG + MXU].astype(F32)
                c = q[0, rows, p * TRIG + MXU:p * TRIG + TRIG].astype(F32)
                u = jnp.where(low64, b, c)
                no = jnp.where(low64, c, b).astype(BF16)
                w = jnp.where(low32, pltpu.roll(u, 96, 1), pltpu.roll(u, 32, 1))
                rot = (u * ct + w * st).astype(BF16)
                Q[HALVES * p, r0:r0 + BL, :LANES] = a
                Q[HALVES * p, r0:r0 + BL, LANES:MXU] = rot
                Q[HALVES * p + 1, r0:r0 + BL, :LANES] = no
                Q[HALVES * p + 1, r0:r0 + BL, LANES:MXU] = rot

    for c in copies(n):
        c.wait()

    WB = 4 * BL
    lane_k = lax.broadcasted_iota(jnp.int32, (WB, LANES), 1)
    KR = wkT.shape[1]

    b0, b1 = tab[n, NB], tab[n, NB + 1]

    @pl.loop(0, NB // 4)
    def _(kc):
        rows = pl.ds(pl.multiple_of(kc * WB, WB), WB)
        blocks = jnp.concatenate([latbuf[tab[n, kc * 4 + j]] for j in range(SOURCES)], axis=0)
        lt = blocks[:, :KR]
        kr = jnp.where(lane_k < HALF, blocks[:, KR:].astype(F32), 0.0)
        krT = kr.T.astype(BF16)
        krO = jnp.concatenate([krT[HALF:], krT[:HALF]], axis=0)
        kt = lax.dot_general(wkT[...], lt, (((1,), (1,)), ((), ())), preferred_element_type=F32).astype(BF16)
        V[rows, :] = jnp.dot(lt, wv[...], preferred_element_type=F32).astype(BF16)
        for h in range(H):
            k = kt[h * LANES:h * LANES + LANES]
            KT[h, :LANES, rows] = k if h % HALVES == 0 else jnp.concatenate([k[HALF:], k[:HALF]], axis=0)
            KT[h, LANES:, rows] = krT if h % HALVES == 0 else krO

    @pl.when(n + 1 < G)
    def _():
        for c in copies(n + 1):
            c.start()

    HR = HALVES * BL
    R = HALVES * HR
    WK = 4 * BL
    row = lax.broadcasted_iota(jnp.int32, (HR, WK), 0)
    col = lax.broadcasted_iota(jnp.int32, (HR, WK), 1)
    dF = jnp.where(row < BL, b0 * BL + row, (b1 - 1) * BL + row) - col
    dS = jnp.where(row < BL, (NB - 1 - b0) * BL + row, (NB - 2 - b1) * BL + row) - col

    nF, nS = NB // 8, NB // 4

    def fold(t):
        w = t.shape[1] // HALVES
        t = jnp.maximum(t[:, :w], t[:, w:])
        return t if w == LANES else fold(t)

    def track(h, part, t, c, count):
        m = fold(t)
        if c > 0:
            m = jnp.maximum(mx[h, part], m)
        if c == count - 1:
            m = jnp.broadcast_to(jnp.max(m, axis=1, keepdims=True), (HR, LANES))
        mx[h, part] = m

    rF, rS = slice(0, HR), slice(HR, R)

    def p1(c, with_f):
        cols = slice(c * WK, c * WK + WK)
        for h in range(H):
            s = jnp.dot(Q[h, 0 if with_f else HR:R, :], KT[h, :, cols], preferred_element_type=F32) * scale2
            if with_f:
                f = jnp.where(dF >= c * WK, s[:HR], NEG)
                sF[h, c] = f
                track(h, rF, f, c, nF)
                s = s[HR:]
            else:
                s = jnp.where(dS >= c * WK, s, NEG)
            sS[h, c] = s
            track(h, rS, s, c, nS)

    def finish(h, part, k, total, l):
        o = (total * (1.0 / jnp.sum(l, axis=1, keepdims=True))).astype(BF16)
        for i in range(HALVES):
            ob[i, k, :, h * LANES:h * LANES + LANES] = o[i * BL:i * BL + BL]

    def p2(c, with_f):
        cols = slice(c * WK, c * WK + WK)
        for h in range(H):
            r0 = 0 if with_f else HR
            es, ls = [], None
            for j in range(WK // LANES):
                js = slice(j * LANES, j * LANES + LANES)
                e = jnp.exp2(sS[h, c, :, js] - mx[h, rS])
                if with_f:
                    e = jnp.concatenate([jnp.exp2(sF[h, c, :, js] - mx[h, rF]), e], axis=0)
                ls = e if ls is None else ls + e
                es.append(e.astype(BF16))
            pv = jnp.dot(jnp.concatenate(es, axis=1), V[cols, h * LANES:h * LANES + LANES], preferred_element_type=F32)
            if c > 0:
                ls, pv = lsum[h, r0:R] + ls, acc[h, r0:R] + pv
            if c == nF - 1:
                finish(h, rF, 0, pv[:HR], ls[:HR])
            if c == nS - 1:
                finish(h, rS, 1, pv, ls)
            else:
                lsum[h, r0:R] = ls
                acc[h, r0:R] = pv

    for k, stage in enumerate((p1, p2)):
        for c in range(nS):
            pl.when(n + c >= -k)(functools.partial(stage, c, c < nF))

    @pl.when(jnp.logical_and(n > 0, n + 1 < G))
    def _():
        for k, f in zip((1, 4), o_forwards(n - 1)):
            o_sends(n - 1)[k].wait_recv()
            f.start()

    for c in o_store(n):
        c.start()

    @pl.when(n == G - 1)
    def _():
        for c in o_store(n):
            c.wait()

        def drain_forward(i, _):
            for f in o_forwards(i):
                f.wait()
            return 0

        @pl.loop(0, G - 1)
        def _(i):
            for k, s in enumerate(o_sends(i)):
                s.wait_send()
                if k in (0, 2, 3):
                    s.wait_recv()

        lax.fori_loop(0, G - 2, drain_forward, 0)
        for k in (1, 4):
            o_sends(G - 2)[k].wait_recv()
        for k, slot in enumerate((me.partner, me.left, me.right)):
            w_send(k, me.c).wait_send()
            w_send(k, slot).wait_recv()


def attention(mesh, tab, q_own, q_par, cs_own, cs_par, wkT, wv, lat, wf, soft_scale):
    G, T = tab.shape[0], q_own.shape[1] * mesh.shape["cp"]
    BL = q_own.shape[1] // HALVES
    NB = T // BL
    VD = wv.shape[1]
    H = VD // LANES
    R = 4 * BL
    dims = (G, NB, BL, H // HALVES, float(soft_scale * LOG2E), mesh.shape["tp"], mesh.shape["cp"])
    blk = lambda a: pl.BlockSpec((1,) + a.shape[1:], lambda n, t: (n, 0, 0))
    full = lambda a: pl.BlockSpec(a.shape, lambda n, t: (0, 0))
    hbm = pl.BlockSpec(memory_space=pltpu.HBM)
    dma = pltpu.SemaphoreType.DMA
    sds = jax.ShapeDtypeStruct
    ost = sds((G, 2, BL, VD), BF16)
    stat = pltpu.VMEM((H, R, LANES), F32)
    return pl.pallas_call(
        functools.partial(attn_kernel, dims),
        grid_spec=pltpu.PrefetchScalarGridSpec(
            num_scalar_prefetch=1, grid=(G,),
            in_specs=[blk(q_own), blk(q_par)] + [pl.BlockSpec((HALVES * BL, cs_own.shape[1]), lambda n, t: (n, 0))] * 2 + [full(wkT), full(wv), hbm, hbm],
            out_specs=[hbm] * 4,
            scratch_shapes=[
                pltpu.VMEM((NB, BL, lat.shape[-1]), BF16), pltpu.VMEM((H, MXU, T), BF16), pltpu.VMEM((T, VD), BF16),
                pltpu.VMEM((H, R, MXU), BF16), pltpu.VMEM((H, NB // 8, R // HALVES, R), F32),
                pltpu.VMEM((H, NB // 4, R // HALVES, R), F32), stat, stat, stat, pltpu.VMEM((2, 2, BL, VD), BF16),
                dma((NB // HALVES,)), dma((HALVES,)), dma((G, 7)), dma((G, 7)), dma((3,)), dma((3,))],
        ),
        out_shape=[ost, ost, sds((4, 2, G, BL, VD), BF16), sds((mesh.shape["cp"],) + wf.shape, BF16)],
        compiler_params=pltpu.CompilerParams(collective_id=1, has_side_effects=True, vmem_limit_bytes=63 * 2**20),
        cost_estimate=pl.CostEstimate(flops=G * H * T * R * 800, bytes_accessed=G * T * 640 * 2, transcendentals=0),
        name="attn",
    )(tab, q_own, q_par, cs_own, cs_par, wkT, wv, lat, wf)


def proj_kernel(dims, x, w_dq, w_dkv, w_uq, g_q, g_kv, cs, w_o,
                lat_all, latent, k_rope, q_own, q_par, wf, cs_par, qn_o, qn_p,
                xbuf, wdq, wdkv, wuq, csb, pay, krb, kvb, qlat, qn, qst, gq, gkv,
                xsem, wsem, csem, osem, wss, wrs, lss, lrs, qss, qrs, css, crs, lsem):
    n_tp, n_cp, n_t, half_cols, wc = dims
    dp, y, c = lax.axis_index("dp"), lax.axis_index("tp"), lax.axis_index("cp")
    core = lax.rem(c, HALVES)
    partner = c + 1 - HALVES * core
    right, left, far = lax.rem(c + 2, n_cp), lax.rem(c + n_cp - 2, n_cp), lax.rem(c + 4, n_cp)
    up, dn, dg = lax.rem(y + 1, n_tp), lax.rem(y + n_tp - 1, n_tp), lax.rem(y + 2, n_tp)
    peers = [(up, c), (dn, c), (dg, c), (y, partner), (y, right), (y, left)]

    barrier = pltpu.get_barrier_semaphore()
    for yy, cc in peers:
        pl.semaphore_signal(barrier, inc=1, device_id=(dp, yy, cc), device_id_type=MESH)
    pl.semaphore_wait(barrier, len(peers))

    def rdma(src, dst, ss, rs, yy, cc):
        return pltpu.make_async_remote_copy(src_ref=src, dst_ref=dst, send_sem=ss, recv_sem=rs,
                                            device_id=(dp, yy, cc), device_id_type=MESH)

    half = lax.rem(y, HALVES)
    col_opp = pl.multiple_of((1 - half) * half_cols + c * wc, LANES)
    col_same = pl.multiple_of(half * half_cols + c * wc, LANES)
    w_sends = [rdma(w_o.at[:, pl.ds(col_opp, wc)], wf.at[0], wss.at[0], wrs.at[0], dn, c),
               rdma(w_o.at[:, pl.ds(col_opp, wc)], wf.at[1], wss.at[1], wrs.at[1], up, c),
               rdma(w_o.at[:, pl.ds(col_same, wc)], wf.at[2], wss.at[2], wrs.at[2], dg, c)]
    for s in w_sends:
        s.start()
    cs_send = rdma(cs, cs_par, css, crs, y, partner)
    cs_send.start()

    rows = xbuf.shape[1]
    bl = pay.shape[3]

    def load_x(i):
        return pltpu.make_async_copy(x.at[pl.ds((i % n_t) * rows, rows), :], xbuf.at[i % HALVES], xsem.at[i % HALVES])

    kr_rank = gkv.shape[1]
    nj = MXU
    loads = [pltpu.make_async_copy(w_dkv, wdkv, wsem.at[0]), pltpu.make_async_copy(g_kv, gkv, wsem.at[1]),
             pltpu.make_async_copy(cs, csb, csem)]
    late = [pltpu.make_async_copy(w_dq, wdq, wsem.at[2]), pltpu.make_async_copy(g_q, gq, wsem.at[3]),
            pltpu.make_async_copy(w_uq.at[:, pl.ds(pl.multiple_of(core * wuq.shape[1], LANES), wuq.shape[1])], wuq, wsem.at[4])]
    loads[0].start()
    load_x(0).start()
    loads[1].start()
    loads[2].start()
    for d in loads:
        d.wait()

    lane = lax.broadcasted_iota(jnp.int32, (rows, LANES), 1)
    low32 = lax.rem(lane, HALF) < 32
    tile = lambda t: pl.ds(t * 2, HALVES)
    stores = {}
    lat_sends = []

    def norm(t32, gain):
        return (t32 * lax.rsqrt(jnp.mean(t32 * t32, axis=-1, keepdims=True) + NORM_EPS) * gain).astype(BF16)

    def send_own(t):
        own = lat_all.at[c, tile(t)]
        for k, cc in ((0, partner), (1, left), (2, right)):
            s = rdma(own, own, lss.at[t, k], lrs.at[t, k], y, cc)
            s.start()
            lat_sends.append(s)

    for t in range(n_t):
        load_x(t).wait()
        if t == 0:
            for d in [load_x(1)] + late:
                d.start()

        def kv_dot(wrows):
            d = lax.dot_general(xbuf[t % HALVES], wdkv[wrows, :], (((1,), (1,)), ((), ())), preferred_element_type=F32)
            return d.astype(BF16)

        @pl.loop(0, kr_rank // nj)
        def _(j):
            kvb[:, pl.ds(pl.multiple_of(j * nj, nj), nj)] = kv_dot(pl.ds(pl.multiple_of(j * nj, nj), nj))

        u = kv_dot(pl.ds(kr_rank, wdkv.shape[0] - kr_rank)).astype(F32)
        load_x(t + 2).start()
        lat = norm(kvb[...].astype(F32), gkv[...])
        u = jnp.concatenate([u, u], axis=1)
        r = pl.ds(t * rows, rows)
        w = jnp.where(low32, pltpu.roll(u, 96, 1), pltpu.roll(u, 32, 1))
        rot = u * csb[r, :LANES] + w * csb[r, LANES:MXU]
        if t >= 2:
            for s in stores.pop(t - 2):
                s.wait()
        sl = t % HALVES
        krb[sl] = rot[:, :HALF].astype(BF16)
        pay[sl, :, :, :, :kr_rank] = lat.reshape(2, 2, bl, kr_rank)
        pay[sl, :, :, :, kr_rank:] = jnp.where(lane < HALF, rot, csb[r, MXU:TRIG]).astype(BF16).reshape(2, 2, bl, LANES)
        st = [pltpu.make_async_copy(pay.at[sl], lat_all.at[c, tile(t)], lsem.at[t]),
              pltpu.make_async_copy(pay.at[sl, :, :, :, :kr_rank], latent.at[tile(t)], osem.at[0, sl]),
              pltpu.make_async_copy(krb.at[sl], k_rope.at[r], osem.at[1, sl])]
        for s in st:
            s.start()
        stores[t] = st[1:]
        if t > 0:
            pltpu.make_async_copy(pay.at[1 - sl], lat_all.at[c, tile(t - 1)], lsem.at[t - 1]).wait()
            send_own(t - 1)

    last = n_t - 1
    for d in late:
        d.wait()

    def stage1(t):
        rp, lp = lat_all.at[right, tile(t)], lat_all.at[left, tile(t)]
        rdma(rp, rp, lss.at[t, 3], lrs.at[t, 1], y, partner).wait_recv()
        rdma(lp, lp, lss.at[t, 3], lrs.at[t, 2], y, partner).wait_recv()
        l0, r1 = lat_all.at[left, tile(t), 0], lat_all.at[right, tile(t), 1]
        for k, src, i, cc in ((5, l0, 5, right), (6, r1, 6, left), (3, rp, 3, partner), (4, lp, 4, partner)):
            s = rdma(src, src, lss.at[t, k], lrs.at[t, i], y, cc)
            s.start()
            lat_sends.append(s)

    def stage2(t):
        f0, f1 = lat_all.at[far, tile(t), 0], lat_all.at[far, tile(t), 1]
        for k, ref in ((5, f0), (6, f1)):
            rdma(ref, ref, lss.at[t, 7], lrs.at[t, k], y, partner).wait_recv()
            s = rdma(ref, ref, lss.at[t, k + 2], lrs.at[t, k + 2], y, partner)
            s.start()
            lat_sends.append(s)

    def project(src, wref, dst, width):
        @pl.loop(0, wref.shape[1] // width)
        def _(j):
            cols = pl.ds(pl.multiple_of(j * width, width), width)
            dst[:, cols] = jnp.dot(src[...], wref[:, cols], preferred_element_type=F32).astype(BF16)

    q_sends, q_stores = [], {}
    for t in range(n_t):
        i = n_t + t
        load_x(i).wait()
        project(xbuf.at[i % HALVES], wdq, qlat, nj)
        if i + 2 < HALVES * n_t:
            load_x(i + 2).start()
        if t == 0:
            sl = last % HALVES
            pltpu.make_async_copy(pay.at[sl], lat_all.at[c, tile(last)], lsem.at[last]).wait()
            send_own(last)
            for k in list(stores):
                for s in stores.pop(k):
                    s.wait()
        stage1(t)
        sl = t % HALVES
        qn[sl] = norm(qlat[...].astype(F32), gq[...])
        r = pl.ds(t * rows, rows)
        cp = pltpu.make_async_copy(qn.at[sl], qn_o.at[r], osem.at[2, sl])
        cp.start()
        if t >= 2:
            q_stores.pop(t - 2).wait()
        project(qn.at[sl], wuq, qst.at[sl], HALVES * nj)
        cp.wait()
        s = rdma(qn_o.at[r], qn_p.at[r], qss.at[t], qrs.at[t], y, partner)
        s.start()
        q_sends.append((cp, s))
        so = pltpu.make_async_copy(qst.at[sl], q_own.at[r], osem.at[3, sl])
        so.start()
        q_stores[t] = so

    def load_qp(t):
        r = pl.ds(t * rows, rows)
        return pltpu.make_async_copy(qn_p.at[r], qn.at[t % HALVES], osem.at[2, t % HALVES])

    def take_qp(t):
        r = pl.ds(t * rows, rows)
        rdma(qn_o.at[r], qn_p.at[r], qss.at[t], qrs.at[t], y, partner).wait_recv()
        load_qp(t).start()

    take_qp(0)
    for t in range(n_t):
        sl = (n_t + t) % HALVES
        for k in [k for k in q_stores if (k % HALVES) == sl]:
            q_stores.pop(k).wait()
        load_qp(t).wait()
        if t + 1 < n_t:
            take_qp(t + 1)
        project(qn.at[t % HALVES], wuq, qst.at[sl], HALVES * nj)
        so = pltpu.make_async_copy(qst.at[sl], q_par.at[pl.ds(t * rows, rows)], osem.at[3, sl])
        so.start()
        q_stores[n_t + t] = so
        stage2(t)
    for k in list(q_stores):
        q_stores.pop(k).wait()

    pp, rp, lp = lax.rem(partner, n_cp), lax.rem(partner + 2, n_cp), lax.rem(partner + n_cp - 2, n_cp)
    fp = lax.rem(partner + 4, n_cp)
    for t in range(n_t):
        for i, ref in ((0, lat_all.at[pp, tile(t)]), (3, lat_all.at[rp, tile(t)]), (4, lat_all.at[lp, tile(t)]),
                       (7, lat_all.at[fp, tile(t), 0]), (8, lat_all.at[fp, tile(t), 1])):
            rdma(ref, ref, lss.at[t, 7], lrs.at[t, i], y, partner).wait_recv()
    for s in lat_sends:
        s.wait_send()
    for _, s in q_sends:
        s.wait_send()
    for s in w_sends:
        s.wait()
    cs_send.wait()


def project_all(mesh, x, w_dq, w_dkv, w_uq, g_q, g_kv, cs, w_o, bl):
    n_tp, n_cp = mesh.shape["tp"], mesh.shape["cp"]
    n_seq, seq, width = x.shape
    rows = HALVES * seq
    n_t = n_seq // HALVES
    rank, kvw = w_dq.shape[1], w_dkv.shape[1]
    kr = g_kv.shape[0]
    qw = w_uq.shape[1] // HALVES
    half_cols = width // HALVES
    wc = half_cols // n_cp
    total = n_seq * seq
    hbm = pl.BlockSpec(memory_space=pltpu.HBM)
    sds = jax.ShapeDtypeStruct
    dma = pltpu.SemaphoreType.DMA
    return pl.pallas_call(
        functools.partial(proj_kernel, (n_tp, n_cp, n_t, half_cols, wc)),
        in_specs=[hbm] * 8,
        out_specs=[hbm] * 9,
        out_shape=[sds((n_cp, n_seq, 2, bl, kr + LANES), BF16), sds((n_seq, 2, bl, kr), BF16), sds((total, kvw - kr), BF16),
                   sds((total, qw), BF16), sds((total, qw), BF16), sds((3, w_o.shape[0], wc), BF16),
                   sds(cs.shape, F32), sds((total, rank), BF16), sds((total, rank), BF16)],
        scratch_shapes=[
            pltpu.VMEM((2, rows, width), BF16), pltpu.VMEM((width, rank), BF16), pltpu.VMEM((kvw, width), BF16),
            pltpu.VMEM((rank, qw), BF16), pltpu.VMEM(cs.shape, F32), pltpu.VMEM((2, 2, 2, bl, kr + LANES), BF16),
            pltpu.VMEM((2, rows, kvw - kr), BF16), pltpu.VMEM((rows, kr), BF16), pltpu.VMEM((rows, rank), BF16), pltpu.VMEM((2, rows, rank), BF16),
            pltpu.VMEM((2, rows, qw), BF16), pltpu.VMEM((1, rank), F32), pltpu.VMEM((1, kr), F32),
            dma((HALVES,)), dma((5,)), dma, dma((4, HALVES)), dma((3,)), dma((3,)), dma((n_t, 9)), dma((n_t, 9)),
            dma((n_t,)), dma((n_t,)), dma, dma, dma((n_t,))],
        compiler_params=pltpu.CompilerParams(collective_id=0, has_side_effects=True, vmem_limit_bytes=63 * 1024 * 1024),
        cost_estimate=pl.CostEstimate(flops=HALVES * total * (width * (rank + kvw) + HALVES * rank * qw), bytes_accessed=10**8,
                                      transcendentals=0),
        name="proj",
    )(x.reshape(total, width), w_dq, w_dkv.T, w_uq, g_q.reshape(1, -1), g_kv.reshape(1, -1), cs, w_o)


def out_kernel(dims, x, w_o, wf, wx, ost_own, ost_par, obuf, out, wy, oy,
               wbuf, ov, xb, stage, wsem, osem, xsem, ssem, oss, ors, wss, wrs, ass, ars):
    n_tp, n_cp, n_seq, bl, half_cols = dims
    me = Place(n_tp, n_cp)
    me.greet(((me.up, me.c), (me.dn, me.c), (me.up, me.partner), (me.dn, me.partner),
              (me.y, me.partner), (me.y, me.right), (me.y, me.left)))
    cols, kb = xb.shape[-1], obuf.shape[-1]
    w, krows = cols // HALVES, w_o.shape[0]
    hk = krows // HALVES
    last = n_seq - 1
    half_of = lambda row: lax.rem(row, HALVES)
    tb = me.block(me.y, me.core)

    to_last = lambda s, p: oy.at[s, p, 1]
    to_prev = lambda s, p: oy.at[s, p, 0]
    prev_fwd = me.o_forwards(lambda s, p: obuf.at[s, p, last - 1], to_prev, oss.at[0], ors.at[0])
    last_sends = me.o_sends(ost_own.at[last], ost_par.at[last], to_last, oss.at[1], ors.at[1])
    last_fwd = me.o_forwards(to_last, to_last, oss.at[1], ors.at[1])
    for s in last_sends + prev_fwd:
        s.start()

    def w_copy(k, src, dst, yy, cc):
        return me.copy(src, dst, wss.at[k], wrs.at[k], yy, cc)

    lo_rows, hi_rows = pl.ds(0, hk), pl.ds(hk, hk)
    p_right, p_left, p_far = (lax.rem(me.partner + k, n_cp) for k in (2, n_cp - 2, n_cp // HALVES))
    w_sends = [w_copy(0, wx.at[me.right], wy.at[me.right], me.y, me.partner), w_copy(1, wx.at[me.left], wy.at[me.left], me.y, me.partner),
               w_copy(2, wx.at[me.left, :, lo_rows], wy.at[me.left, :, lo_rows], me.y, me.right),
               w_copy(3, wx.at[me.right, :, hi_rows], wy.at[me.right, :, hi_rows], me.y, me.left)]
    for s in w_sends:
        s.start()
    far_fwd = []
    for k, part in ((4, lo_rows), (5, hi_rows)):
        ref = wy.at[me.far, :, part]
        far_fwd.append(w_copy(k, ref, ref, me.y, me.partner))

    def w_recv(k, ref):
        w_copy(k, ref, ref, me.y, me.partner).wait_recv()

    n_m = n_seq // HALVES
    rows = HALVES * bl
    k_of = (None, me.flip, 1 - me.flip, HALVES)
    pieces = ((wf, wx.at[me.partner]), (wx.at[me.right], wy.at[p_right]), (wx.at[me.left], wy.at[p_left]), (wy.at[me.far], wy.at[p_far]))
    offs = [pl.multiple_of(v * w, LANES) for v in (me.core, 1 - me.core)]

    def col_of(j, row):
        dx = j + (j // HALVES) * (1 - HALVES * (j % HALVES))
        xq = lax.rem(lax.div(me.c, HALVES) + dx, n_cp // HALVES)
        return pl.multiple_of(half_of(row) * half_cols + xq * cols, LANES)

    def w_loads(j):
        b = j % HALVES
        out_ = [pltpu.make_async_copy(w_o.at[:, pl.ds(col_of(j, me.y), cols)], wbuf.at[b, 0], wsem.at[b, 0])]
        for r in range(1, 4):
            for part in range(HALVES):
                out_.append(pltpu.make_async_copy(pieces[j][part].at[k_of[r]], wbuf.at[b, r, :, pl.ds(offs[part], w)],
                                                  wsem.at[b, HALVES * r + part]))
        return out_

    def x_load(j):
        return pltpu.make_async_copy(x.at[:, pl.ds(pl.multiple_of(tb * bl, bl), bl), pl.ds(col_of(j, me.y), cols)], xb.at[j % HALVES], xsem.at[j % HALVES])

    o_offs = [pl.multiple_of(v * kb, LANES) for v in (me.core, 1 - me.core)]

    def o_loads(n0, cnt, refs):
        out_ = []
        for i in range(cnt):
            for r in range(SOURCES):
                for part in range(HALVES):
                    src = ost_own.at[n0 + i, tb] if (r, part) == (0, 0) else refs(r, part, n0 + i)
                    out_.append(pltpu.make_async_copy(src, ov.at[n0 + i, :, pl.ds(pl.multiple_of(r * krows + o_offs[part], LANES), kb)],
                                                      osem.at[n0 + i, HALVES * r + part]))
        return out_

    early = o_loads(0, last - 1, lambda r, p, i: obuf.at[r, p, i])
    late = o_loads(last - 1, 2, lambda r, p, i: oy.at[r, p, i - last + 1] if (i == last or r == 3) else obuf.at[r, p, i])
    for d in w_loads(0) + early + [x_load(0)]:
        d.start()

    def region(row, j, m, n0=0, cnt=2):
        return out.at[pl.ds(HALVES * m + n0, cnt), pl.ds(pl.multiple_of(me.block(row, me.core) * bl, bl), bl), pl.ds(col_of(j, row), cols)]

    def ring(k, ref, j, m, yy):
        i = j * n_m + m
        return me.copy(ref, ref, ass.at[i, k], ars.at[i, k], yy, me.c)

    def tile_sends(j, m):
        ref = region(me.y, j, m)
        return ring(0, ref, j, m, me.up), ring(1, ref, j, m, me.dn)

    def forward(j, m):
        ring(0, region(me.dn, j, m), j, m, me.up).wait_recv()
        ring(2, region(me.dn, j, m, 0, 1), j, m, me.up).start()
        ring(1, region(me.up, j, m), j, m, me.up).wait_recv()
        ring(3, region(me.up, j, m, 1, 1), j, m, me.dn).start()

    nt = MXU

    def tile(j, m):
        b = j % HALVES

        @pl.loop(0, cols // nt)
        def _(t):
            cs_ = pl.ds(pl.multiple_of(t * nt, nt), nt)
            a = ov[pl.ds(HALVES * m, HALVES)].reshape(rows, 4 * krows)
            s = None
            for r in range(SOURCES):
                d = jnp.dot(a[:, r * krows:(r + 1) * krows], wbuf[b, r, :, cs_], preferred_element_type=F32)
                s = d if s is None else s + d
            xr = xb[b, pl.ds(HALVES * m, HALVES), :, cs_].reshape(rows, nt).astype(F32)
            stage[:, :, cs_] = (xr + s).astype(BF16).reshape(2, bl, nt)

        c = pltpu.make_async_copy(stage, region(me.y, j, m), ssem)
        c.start()
        c.wait()
        for s in tile_sends(j, m):
            s.start()

    def need(j):
        if j == 0:
            w_recv(0, wy.at[p_right])
        elif j == 1:
            w_recv(1, wy.at[p_left])
        else:
            for k, part in ((2, lo_rows), (3, hi_rows)):
                w_recv(k, wy.at[me.far, :, part])
            for f in far_fwd:
                f.start()
            for k, part in ((4, lo_rows), (5, hi_rows)):
                w_recv(k, wy.at[p_far, :, part])
        for d in w_loads(j + 1) + [x_load(j + 1)]:
            d.start()

    def late_o():
        for k, f in zip((1, 4), last_fwd):
            last_sends[k].wait_recv()
            f.start()
        for k in (0, 2, 3):
            last_sends[k].wait_recv()
        for f in prev_fwd + last_fwd:
            f.wait_recv()
        for d in late:
            d.start()
        for d in late:
            d.wait()

    for d in early:
        d.wait()

    @pl.loop(0, 4 * n_m)
    def _(i):
        j, m = lax.div(i, n_m), lax.rem(i, n_m)
        for jj in range(SOURCES):
            @pl.when(i == jj * n_m)
            def _(jj=jj):
                for d in w_loads(jj) + [x_load(jj)]:
                    d.wait()
                if jj < 2:
                    need(jj)
        pl.when(i == n_m - 1)(late_o)
        tile(j, m)

        @pl.when(j > 0)
        def _():
            forward(j - 1, m)

        pl.when(i == 3 * n_m - 1)(lambda: need(2))

    @pl.loop(0, n_m)
    def _(m):
        forward(3, m)

    @pl.loop(0, 4 * n_m)
    def _(i):
        j, m = lax.div(i, n_m), lax.rem(i, n_m)
        for k, row, n0, cnt in ((0, me.y, 0, HALVES), (1, me.y, 0, HALVES), (2, me.dn, 0, 1), (3, me.up, 1, 1)):
            r = region(row, j, m, n0, cnt)
            me.copy(r, r, ass.at[i, k], ars.at[i, k], me.up, me.c).wait_send()
        for k, n0 in ((2, 0), (3, 1)):
            r = region(me.dg, j, m, n0, 1)
            me.copy(r, r, ass.at[i, k], ars.at[i, k], me.up, me.c).wait_recv()

    for s in last_sends + prev_fwd + last_fwd + w_sends + far_fwd:
        s.wait_send()


def out_product(mesh, x, w_o, wf, wx, ost_own, ost_par, obuf):
    n_tp, n_cp = mesh.shape["tp"], mesh.shape["cp"]
    n_seq, seq, width = x.shape
    bl = seq // HALVES
    cols = HALVES * wf.shape[-1]
    krows = w_o.shape[0]
    hbm = pl.BlockSpec(memory_space=pltpu.HBM)
    dma = pltpu.SemaphoreType.DMA
    sds = jax.ShapeDtypeStruct
    tiles = HALVES * n_seq
    return pl.pallas_call(
        functools.partial(out_kernel, (n_tp, n_cp, n_seq, bl, width // HALVES)),
        in_specs=[hbm] * 7, out_specs=[hbm] * 3,
        out_shape=[sds(x.shape, BF16), sds(wx.shape, BF16), sds((4, 2, HALVES) + obuf.shape[3:], BF16)],
        scratch_shapes=[
            pltpu.VMEM((2, 4, krows, cols), BF16), pltpu.VMEM((n_seq, bl, 4 * krows), BF16), pltpu.VMEM((2, n_seq, bl, cols), BF16),
            pltpu.VMEM((2, bl, cols), BF16), dma((2, 8)), dma((n_seq, 8)), dma((HALVES,)), dma, dma((2, 7)), dma((2, 7)),
            dma((6,)), dma((6,)), dma((tiles, 4)), dma((tiles, 4))],
        compiler_params=pltpu.CompilerParams(collective_id=2, has_side_effects=True, vmem_limit_bytes=63 * 2**20),
        cost_estimate=pl.CostEstimate(flops=n_seq * seq * cols * 16 * krows, bytes_accessed=10**8, transcendentals=0),
        name="outp",
    )(x, w_o, wf, wx, ost_own, ost_par, obuf)[0]


def settle_kernel(src, dst, buf, rsem, wsem):
    n = buf.shape[0]
    ins = [pltpu.make_async_copy(src.at[i], buf.at[i], rsem.at[i]) for i in range(n)]
    outs = [pltpu.make_async_copy(buf.at[i], dst.at[i], wsem.at[i]) for i in range(n)]
    for d in ins:
        d.start()
    for a, b in zip(ins, outs):
        a.wait()
        b.start()
    for b in outs:
        b.wait()


def settle(a):
    parts = HALVES * a.shape[0]
    shape = (parts, a.shape[1] // HALVES, a.shape[2])
    hbm = pl.BlockSpec(memory_space=pltpu.HBM)
    sem = pltpu.SemaphoreType.DMA((parts,))
    return pl.pallas_call(
        settle_kernel, in_specs=[hbm], out_specs=hbm, out_shape=jax.ShapeDtypeStruct(shape, a.dtype),
        scratch_shapes=[pltpu.VMEM(shape, a.dtype), sem, sem],
        compiler_params=pltpu.CompilerParams(vmem_limit_bytes=32 * 2**20), name="settle",
    )(a.reshape(shape)).reshape(a.shape)


ROPE_BASE = 10000.0


def solution(mesh):
    def local_step(x, pos, w_dq, g_q, w_uq, w_dkv, g_kv, w_uk, w_uv, w_o):
        n_seq, seq, _ = x.shape
        n_cp = mesh.shape["cp"]
        bl = seq // HALVES
        nb = HALVES * n_cp
        kv_rank = g_kv.shape[0]
        rope = w_dkv.shape[1] - kv_rank
        heads = (w_uq.shape[1] - w_uk.shape[1]) // rope
        nope = w_uk.shape[1] // heads
        c = lax.axis_index("cp")
        core = c % HALVES

        inv_freq = ROPE_BASE ** (-2.0 * jnp.arange(rope // HALVES, dtype=F32) / rope)
        lanes = jnp.arange(LANES)
        ang = pos.astype(F32)[..., None] * jnp.tile(inv_freq, LANES // (rope // HALVES))
        sign = jnp.where(lanes % rope < rope // HALVES, -1.0, 1.0)
        bid = jnp.broadcast_to((pos[:, :1] // bl).astype(F32)[..., None], ang.shape)
        cs_own = jnp.concatenate([jnp.cos(ang), jnp.sin(ang) * sign, bid], axis=-1).reshape(n_seq * seq, TRIG)
        lat_all, latent, k_rope, q_own, q_par, wf, cs_par, _, _ = project_all(
            mesh, x, w_dq, w_dkv, w_uq, g_q, g_kv, cs_own, w_o, bl)
        latent, k_rope = latent.reshape(n_seq, seq, kv_rank), k_rope.reshape(n_seq, seq, rope)
        q_own, q_par = (a.reshape(n_seq, seq, -1) for a in (q_own, q_par))
        hw = w_uk.shape[1] // HALVES
        wkT = lax.dynamic_slice(w_uk, (0, core * hw), (kv_rank, hw)).T
        wv = lax.dynamic_slice(w_uv, (0, core * hw), (kv_rank, hw))

        ids = lat_all[:, :, 0, 0, kv_rank + rope].astype(jnp.int32)
        blocks = jnp.arange(nb)
        first = ids[:, :, None] == blocks
        second = nb - 1 - ids[:, :, None] == blocks
        dev = jnp.arange(n_cp)[:, None, None]
        slots = jnp.sum(jnp.where(first, HALVES * dev, 0) + jnp.where(second, HALVES * dev + 1, 0), axis=0)
        mine = [jnp.sum(jnp.where(jnp.arange(n_cp)[:, None] == k, ids, 0), axis=0)[:, None] for k in (c, c ^ 1)]
        tab = jnp.concatenate([slots] + mine, axis=1).astype(jnp.int32)

        ost_own, ost_par, obuf, wx = attention(mesh, tab, q_own, q_par, cs_own, cs_par, wkT, wv, lat_all, wf, (nope + rope) ** -0.5)
        return settle(out_product(mesh, x, w_o, wf, wx, ost_own, ost_par, obuf)), latent, k_rope

    seq_spec = P("dp", "cp", None)
    whole = P(None, None)
    in_specs = (seq_spec, P("dp", "cp"), whole, P(None), P(None, "tp"), whole, P(None), P(None, "tp"), P(None, "tp"), P("tp", None))
    return jax.shard_map(local_step, mesh=mesh, in_specs=in_specs, out_specs=(seq_spec,) * 3, check_vma=False)
```

time: 1310 us -> 426 us (0.33)
  waiting for transfers between devices: 759 us -> 0 us
  matrix products: 440 us -> 0 us
  Pallas kernels: 0 us -> 398 us
  other arithmetic: 38.4 us -> 8.81 us
  blocking collectives: 21.9 us -> 0 us
  local copies, waits for them, and re-layouts: 31.1 us -> 14.1 us
  between operations: 14.4 us -> 1.2 us
    psum x1 -> x0, waiting for transfers between devices: 625 us -> none  [local_step(): head_sum = lax.psum(part_out, 'tp')]
    pallas_call x0 -> x4, Pallas kernels: none -> 398 us  [the longest x1 189 us: out_product(): pl.pallas_call(functools.partial(out_kernel, (n_tp, n_cp, n_seq, bl, widt...]
    dot_general x8 -> x0, matrix products: 279 us -> none  [the longest x1 78.8 us: attend(): jnp.einsum('nhst,nthd->nshd', probs_bf, values, preferred_element_type=jn...]
    sub x1 -> x0, matrix products: 161 us -> none  [attend(): probs_bf = jax.nn.softmax(scores, axis=-1).astype(jnp.bfloat16)]
    all_gather x3 -> x0, waiting for transfers between devices: 134 us -> none  [the longest x1 74.8 us: local_step(): values_all = lax.all_gather(values, 'cp', axis=1, tiled=True)]
    convert_element_type x5 -> x3, other arithmetic: 30.3 us -> 3.55 us  [the longest x1 1.9 us: local_step(): ids = lat_all[:, :, 0, 0, kv_rank + rope].astype(jnp.int32)]
    all_gather x1 -> x0, blocking collectives: 21.9 us -> none  [local_step(): pos_all = lax.all_gather(pos_blk, 'cp', axis=1, tiled=True)]
  transfers between devices with their start and end apart: 4 -> 0, of which waited for: 3 -> 0; matrix products, arithmetic and copies ran while one was open for 26% -> 0% of each run, Pallas kernels for 0% -> 0%
where the time goes in v1:
time: 426 us; the launch traced here: 422 us
  Pallas kernels  398 us (93%)
  local copies, waits for them, and re-layouts  14.1 us (3%)
  other arithmetic  8.81 us (2%)
    pallas_call x1, Pallas kernels, out_product(): pl.pallas_call(functools.partial(out_kernel, (n_tp, n_cp, n_seq, bl, widt...  189 us
    pallas_call x1, Pallas kernels, attention(): pl.pallas_call(functools.partial(attn_kernel, dims), grid_spec=pltpu.Pref...  109 us
    pallas_call x1, Pallas kernels, project_all(): pl.pallas_call(functools.partial(proj_kernel, (n_tp, n_cp, n_t, half_cols...  92 us
    unnamed x11, local copies, waits for them, and re-layouts  10.8 us

profile of v1, /device:TPU:97, one launch (start us, length us, event | category | flops | bytes accessed | tf_op | source)
XLA Modules:
  0.0 422.4 jit_solution(12748731264334790662)
XLA Ops:
  0.6 0.0 copy-start.2
  0.7 1.0 fusion.3
  1.7 0.1 mul.51
  1.7 1.3 reshape.91.g_q
  3.0 0.1 broadcast_in_dim.74
  3.1 0.7 convert_element_type.19
  3.8 0.0 copy-start.3
  3.8 0.3 broadcast_in_dim.76
  4.1 2.8 multiply_cosine_fusion
  6.9 1.6 pad_maximum_fusion.cs.refs_2_
  8.5 0.0 copy-done.2
  8.5 0.0 copy-done.3
  8.5 1.2 constant_dynamic-slice_fusion
  9.7 1.5 copy.27
  11.2 92.0 %proj.1 = (bf16[8,6,2,128,640]{4,3,2,1,0:T(8,128)(2,1)}, bf16[6,2,128,512]{3,2,1,0:T(8,128)(2,1)}, bf16[1536,64]{1,0:T(8,128)(2,1)}, bf16[1536,1536]{1,0:T(8,128...) custom-call(bf16[1536,6144]{1,0:T(8,128)(2,1)} %bitcast.19, ...), custom_call_target="tpu_custom_call" | custom-call | flops 54358179840 | bytes 100000000 | tf_op jit(solution)/shard_map/proj/pallas_call | solution.py:508
  103.2 1.9 convert_reduce_fusion
  105.1 0.1 copy.21
  105.2 0.1 select_reduce_fusion.1
  105.3 0.1 copy.24
  105.4 0.1 copy.23
  105.5 0.1 copy.22
  105.6 0.1 add_reduce_fusion
  105.7 0.7 pad_add_fusion.tab
  106.3 1.8 copy.26
  108.2 108.9 %attn.1 = (bf16[6,2,128,1024]{3,2,1,0:T(8,128)(2,1)}, bf16[6,2,128,1024]{3,2,1,0:T(8,128)(2,1)}, bf16[4,2,6,128,1024]{4,3,2,1,0:T(8,128)(2,1)}, bf16[8,3,2048,384]{3,2,1,0:T(8,128)(2,1)}) custom-call(s32[6,18]{1,0:T(8,128)} %pad_add_fusion.tab, bf16[6,256,1536]{2,1,0:T(8,128)(2,1)} %bitcast.22, bf16[6,256,1536]{2,1,0:T(8,128)(2,1)} %bitcast.23, ...), custom_call_target="tpu_custom_call" | custom-call | flops 40265318400 | bytes 15728640 | tf_op jit(solution)/shard_map/attn/pallas_call | solution.py:271
  217.1 189.3 %outp.1 = (bf16[6,256,6144]{2,1,0:T(8,128)(2,1)}, bf16[8,3,2048,384]{3,2,1,0:T(8,128)(2,1)}, bf16[4,2,2,128,1024]{4,3,2,1,0:T(8,128)(2,1)}) custom-call(bf16[6,256,6144]{2,1,0:T(8,128)(2,1)} %x.1, bf16[2048,6144]{1,0:T(8,128)(2,1)} %w_o.3, bf16[3,2048,384]{2,1,0:T(8,128)(2,1)} %get-tuple-element.15.refs_7_.wf, ...), custom_call_target="tpu_custom_call" | custom-call | flops 38654705664 | bytes 100000000 | tf_op jit(solution)/shard_map/outp/pallas_call | solution.py:725
  406.4 0.0 copy-start
  406.5 6.4 %copy-done = bf16[6,256,6144]{2,1,0:T(8,128)(2,1)S(1)} copy-done((bf16[6,256,6144]{2,1,0:T(8,128)(2,1)S(1)}, bf16[6,256,6144]{2,1,0:T(8,128)(2,1)}, u32[]{:S(2)}) %copy-start) | copy-done | bytes 18874392
  412.8 0.0 copy-start.1
  412.8 7.9 %settle.1 = bf16[12,128,6144]{2,1,0:T(8,128)(2,1)} custom-call(bf16[12,128,6144]{2,1,0:T(8,128)(2,1)S(1)} %bitcast.12), custom_call_target="tpu_custom_call" | custom-call | tf_op jit(solution)/shard_map/settle/pallas_call | solution.py:757
  420.8 0.0 copy-done.1
  420.8 1.1 copy.29
  (7 shorter events, 0.0 us)
Async XLA Ops:
  0.6 7.8 %copy-start.2 = (bf16[512,2048]{1,0:T(8,128)(2,1)S(1)}, bf16[512,2048]{1,0:T(8,128)(2,1)}, u32[]{:S(2)}) copy-start(bf16[512,2048]{1,0:T(8,128)(2,1)} %param.18) | copy-start | bytes 6291460
  3.8 4.7 %copy-start.3 = (bf16[512,2048]{1,0:T(8,128)(2,1)S(1)}, bf16[512,2048]{1,0:T(8,128)(2,1)}, u32[]{:S(2)}) copy-start(bf16[512,2048]{1,0:T(8,128)(2,1)} %param.17) | copy-start | bytes 6291460
  406.4 6.4 %copy-start = (bf16[6,256,6144]{2,1,0:T(8,128)(2,1)S(1)}, bf16[6,256,6144]{2,1,0:T(8,128)(2,1)}, u32[]{:S(2)}) copy-start(bf16[6,256,6144]{2,1,0:T(8,128)(2,1)} %get-tuple-element.24) | copy-start | bytes 56623108
  412.8 8.0 %copy-start.1 = (bf16[6,2,128,512]{3,2,1,0:T(8,128)(2,1)S(1)}, bf16[6,2,128,512]{3,2,1,0:T(8,128)(2,1)}, u32[]{:S(2)}) copy-start(bf16[6,2,128,512]{3,2,1,0:T(8,128)(2,1)} %get-tuple-element.25) | copy-start | bytes 4718596

commit v2 on v1

v2 whole, which is shorter than its diff:
```python
import functools
import numpy as np
import jax, jax.numpy as jnp
from jax import lax
from jax.experimental import pallas as pl
from jax.experimental.pallas import tpu as pltpu
from jax.sharding import PartitionSpec as P

F32, BF16 = jnp.float32, jnp.bfloat16
NEG = float("-inf")
LOG2E = 1.4426950408889634
LANES, HALF, QUARTER, MXU, WIDE, PAIR = 128, 64, 32, 256, 512, 384
HALVES = 2
SOURCES = 4
MIB = 2**20
SPARE = 7


MESH = pl.DeviceIdType.MESH
NORM_EPS = 1e-6


class Place:
    def __init__(self, n_tp, n_cp):
        self.dp, self.y, self.c = (lax.axis_index(a) for a in ("dp", "tp", "cp"))
        y, c = self.y, self.c
        self.n_tp = n_tp
        self.core = lax.rem(c, HALVES)
        self.partner = c + 1 - HALVES * self.core
        self.right, self.left, self.far = (lax.rem(c + k, n_cp) for k in (HALVES, n_cp - 2, n_cp // HALVES))
        self.up, self.dn, self.dg = (lax.rem(y + k, n_tp) for k in (1, n_tp - 1, n_tp // HALVES))
        self.flip = lax.rem(y + self.core, HALVES)
        self.mate = lax.rem(y + 1 + HALVES * self.flip, n_tp)
        self.other = lax.rem(y + 3 - HALVES * self.flip, n_tp)

    def block(self, row, core):
        return lax.div(lax.rem(row + (self.n_tp - 1) * core, self.n_tp), HALVES)

    def greet(self, peers):
        barrier = pltpu.get_barrier_semaphore()
        for yy, cc in peers:
            pl.semaphore_signal(barrier, inc=1, device_id=(self.dp, yy, cc), device_id_type=MESH)
        pl.semaphore_wait(barrier, len(peers))

    def copy(self, src, dst, ss, rs, yy, cc):
        return pltpu.make_async_remote_copy(src_ref=src, dst_ref=dst, send_sem=ss, recv_sem=rs,
                                            device_id=(self.dp, yy, cc), device_id_type=MESH)

    def o_sends(self, own, par, dst, ss, rs):
        tb, tp = self.block(self.y, self.core), self.block(self.y, 1 - self.core)
        ways = [(own, tb, 1, 0, self.mate, self.c), (own, 1 - tb, 2, 0, self.other, self.c), (par, tp, 0, 1, self.y, self.partner),
                (par, tp, 1, 1, self.other, self.partner), (par, 1 - tp, 2, 1, self.mate, self.partner)]
        return [self.copy(a.at[blk], dst(src, part), ss.at[k], rs.at[k], yy, cc)
                for k, (a, blk, src, part, yy, cc) in enumerate(ways)]

    def o_forwards(self, src, dst, ss, rs):
        return [self.copy(src(2, part), dst(3, part), ss.at[5 + part], rs.at[5 + part], self.mate, self.c) for part in range(HALVES)]


def w_parts(rows):
    cut = rows // 8
    return (pl.ds(0, rows - cut), pl.ds(cut, rows - cut)), (pl.ds(rows - cut, cut), pl.ds(0, cut))


def attn_kernel(dims, tab, *refs):
    G, NB, BL, HP, scale2, n_tp, n_cp = dims
    CK = HALVES * BL
    H = HALVES * HP
    q_own, q_par, cs_own, cs_par, w_uk, w_uv, lat, wf = refs[:8]
    ost_own, ost_par, obuf, wx = refs[8:12]
    latbuf, KT, V, Q, sF, sS, sX, mx, lsum, acc, ob, wk, wkT, wv, sem, ksem, osem, oss, ors, wss, wrs = refs[12:]
    n = pl.program_id(0)
    me = Place(n_tp, n_cp)
    rows_ = ((me.up, me.c), (me.dn, me.c), (me.up, me.partner), (me.dn, me.partner))
    w_to = ((me.y, me.partner), (me.y, me.right), (me.y, me.left))

    krows = wf.shape[1]
    w_rows = (pl.ds(0, krows),) + w_parts(krows)[0]

    def w_send(k, slot):
        return me.copy(wf.at[:, w_rows[k]], wx.at[slot, :, w_rows[k]], wss.at[k], wrs.at[k], *w_to[k])

    def copies(i):
        return [pltpu.make_async_copy(lat.at[p, i], latbuf.at[pl.ds(HALVES * p, HALVES)], sem.at[p]) for p in range(n_cp)]

    def o_store(i):
        return [pltpu.make_async_copy(ob.at[k], dst.at[i], osem.at[k]) for k, dst in enumerate((ost_own, ost_par))]

    def o_sends(i):
        return me.o_sends(ost_own.at[i], ost_par.at[i], lambda s, p: obuf.at[s, p, i], oss.at[i], ors.at[i])

    def o_forwards(i):
        at = lambda s, p: obuf.at[s, p, i]
        return me.o_forwards(at, at, oss.at[i], ors.at[i])

    hw = wv.shape[1]
    kv_loads = [pltpu.make_async_copy(a.at[:, pl.ds(pl.multiple_of(me.core * hw, LANES), hw)], b, ksem.at[k])
                for k, (a, b) in enumerate(((w_uk, wk), (w_uv, wv)))]

    @pl.when(n == 0)
    def _():
        for c in copies(0) + kv_loads:
            c.start()
        me.greet(rows_ + w_to)
        for k in range(3):
            w_send(k, me.c).start()
        for c in kv_loads:
            c.wait()
        wkT[...] = wk[...].T

    lane = lax.broadcasted_iota(jnp.int32, (BL, LANES), 1)
    low64 = lane < HALF
    low32 = lax.rem(lane, HALF) < QUARTER
    for src_i, (q, cs) in enumerate(((q_own, cs_own), (q_par, cs_par))):
        @pl.loop(0, HALVES)
        def _(half, src_i=src_i, q=q, cs=cs):
            r0 = half * 2 + src_i
            rows = pl.ds(pl.multiple_of(half * BL, BL), BL)
            ct = cs[rows, :LANES]
            st = cs[rows, LANES:]
            for p in range(HP):
                a = q[0, rows, p * PAIR:p * PAIR + LANES]
                b = q[0, rows, p * PAIR + LANES:p * PAIR + MXU].astype(F32)
                c = q[0, rows, p * PAIR + MXU:p * PAIR + PAIR].astype(F32)
                u = jnp.where(low64, b, c)
                no = jnp.where(low64, c, b).astype(BF16)
                w = jnp.where(low32, pltpu.roll(u, 96, 1), pltpu.roll(u, QUARTER, 1))
                rot = (u * ct + w * st).astype(BF16)
                Q[HALVES * p, r0, :, :LANES] = a
                Q[HALVES * p, r0, :, LANES:MXU] = rot
                Q[HALVES * p + 1, r0, :, :LANES] = no
                Q[HALVES * p + 1, r0, :, LANES:MXU] = rot

    @pl.when(n > 0)
    def _():
        for c in o_store(n - 1):
            c.wait()
        for s in o_sends(n - 1):
            s.start()

    for c in copies(n):
        c.wait()

    WB = 4 * BL
    lane_k = lax.broadcasted_iota(jnp.int32, (WB, LANES), 1)
    KR = wkT.shape[1]

    b0, b1 = tab[n, NB], tab[n, NB + 1]

    @pl.loop(0, NB // 4)
    def _(kc):
        blocks = jnp.concatenate([latbuf[tab[n, kc * 4 + j]] for j in range(SOURCES)], axis=0)
        lt = blocks[:, :KR]
        kr = jnp.where(lane_k < HALF, blocks[:, KR:].astype(F32), 0.0)
        krT = kr.T.astype(BF16)
        krO = jnp.concatenate([krT[HALF:], krT[:HALF]], axis=0)
        kt = lax.dot_general(wkT[...], lt, (((1,), (1,)), ((), ())), preferred_element_type=F32).astype(BF16)
        V[kc] = jnp.dot(lt, wv[...], preferred_element_type=F32).astype(BF16)
        for h in range(H):
            k = kt[h * LANES:h * LANES + LANES]
            KT[kc, h, :LANES] = k if h % HALVES == 0 else jnp.concatenate([k[HALF:], k[:HALF]], axis=0)
            KT[kc, h, LANES:] = krT if h % HALVES == 0 else krO

    @pl.when(n + 1 < G)
    def _():
        for c in copies(n + 1):
            c.start()

    HR = HALVES * BL
    R = HALVES * HR
    WK = 4 * BL
    nS = NB // 4 - 1
    row = lax.broadcasted_iota(jnp.int32, (HR, WK), 0)
    col = lax.broadcasted_iota(jnp.int32, (HR, WK), 1)
    dF = jnp.where(row < BL, b0 * BL + row, (b1 - 1) * BL + row) - col
    dS = jnp.where(row < BL, (NB - 1 - b0) * BL + row, (NB - 2 - b1) * BL + row) - col
    rF, rS = slice(0, HR), slice(HR, R)
    extra = []
    for i in range(HALVES):
        at = [tab[n, NB + 2 + 4 * i + k] for k in range(SOURCES)]
        is_first = row[:BL, :LANES] * 0 + at[3] > 0
        extra.append((at[0], at[1], row[:BL] + at[2] - col[:BL], is_first, pl.ds(i * BL, BL), pl.ds((2 + i) * BL, BL)))

    def fold(t):
        w = t.shape[1] // HALVES
        t = jnp.maximum(t[:, :w], t[:, w:])
        return t if w == LANES else fold(t)

    def p1(c):
        for h in range(H):
            q = Q[h, 2:].reshape(HR, MXU) if c else Q[h].reshape(R, MXU)
            s = jnp.dot(q, KT[c, h], preferred_element_type=F32) * scale2
            if c == 0:
                f = jnp.where(dF >= 0, s[:HR], NEG)
                sF[h] = f
                mx[h, rF] = fold(f)
                s = s[HR:]
            elif c == nS - 1:
                s = jnp.where(dS >= c * WK, s, NEG)
            sS[h, c] = s
            mx[h, rS] = jnp.maximum(mx[h, rS], fold(s)) if c else fold(s)

    def p1x():
        for h in range(H):
            for i, (block, chunk, d, is_first, r_f, r_s) in enumerate(extra):
                s = jnp.dot(Q[h, block], KT[chunk, h], preferred_element_type=F32) * scale2
                s = jnp.where(d >= 0, s, NEG)
                sX[h, i] = s
                m = fold(s)
                for r, t in ((r_f, jnp.where(is_first, m, NEG)), (r_s, jnp.where(is_first, NEG, m))):
                    t = jnp.maximum(mx[h, r], t)
                    mx[h, r] = jnp.broadcast_to(jnp.max(t, axis=1, keepdims=True), (BL, LANES))

    def weigh(load, chunk, h):
        es, ls = [], None
        for j in range(WK // LANES):
            e = jnp.exp2(load(slice(j * LANES, j * LANES + LANES)))
            ls = e if ls is None else ls + e
            es.append(e.astype(BF16))
        return ls, jnp.dot(jnp.concatenate(es, axis=1), V[chunk, :, h * LANES:h * LANES + LANES], preferred_element_type=F32)

    def p2(c):
        for h in range(H):
            def load(js):
                t = sS[h, c, :, js] - mx[h, rS]
                return t if c else jnp.concatenate([sF[h, :, js] - mx[h, rF], t], axis=0)
            ls, pv = weigh(load, c, h)
            r = rS if c else slice(0, R)
            lsum[h, r] = lsum[h, r] + ls if c else ls
            acc[h, r] = acc[h, r] + pv if c else pv

    def p2x():
        for h in range(H):
            for i, (_, chunk, _, is_first, r_f, r_s) in enumerate(extra):
                m = jnp.where(is_first, mx[h, r_f], mx[h, r_s])
                ls, pv = weigh(lambda js: sX[h, i, :, js] - m, chunk, h)
                for k, r in enumerate((r_f, r_s)):
                    pick = (lambda t: jnp.where(is_first, t, 0.0)) if k == 0 else (lambda t: jnp.where(is_first, 0.0, t))
                    l = lsum[h, r] + pick(ls)
                    total = acc[h, r] + pick(pv)
                    ob[i, k, :, h * LANES:h * LANES + LANES] = (total * (1.0 / jnp.sum(l, axis=1, keepdims=True))).astype(BF16)

    stages = [functools.partial(f, c) for f in (p1, p2) for c in range(nS)]
    stages.insert(nS, p1x)
    for k, stage in enumerate(stages + [p2x]):
        pl.when(n + k >= 0)(stage)

    @pl.when(jnp.logical_and(n > 0, n + 1 < G))
    def _():
        for k, f in zip((1, 4), o_forwards(n - 1)):
            o_sends(n - 1)[k].wait_recv()
            f.start()

    for c in o_store(n):
        c.start()

    @pl.when(n == G - 1)
    def _():
        for c in o_store(n):
            c.wait()

        def drain_forward(i, _):
            for f in o_forwards(i):
                f.wait()
            return 0

        @pl.loop(0, G - 1)
        def _(i):
            for k, s in enumerate(o_sends(i)):
                s.wait_send()
                if k in (0, 2, 3):
                    s.wait_recv()

        lax.fori_loop(0, G - 2, drain_forward, 0)
        for k in (1, 4):
            o_sends(G - 2)[k].wait_recv()
        for k, slot in enumerate((me.partner, me.left, me.right)):
            w_send(k, me.c).wait_send()
            w_send(k, slot).wait_recv()


def attention(mesh, tab, q_own, q_par, cs_own, cs_par, w_uk, w_uv, lat, wf, soft_scale):
    G, T = tab.shape[0], q_own.shape[1] * mesh.shape["cp"]
    BL = q_own.shape[1] // HALVES
    NB = T // BL
    KR, VD = w_uv.shape[0], w_uv.shape[1] // HALVES
    H = VD // LANES
    R = 4 * BL
    dims = (G, NB, BL, H // HALVES, float(soft_scale * LOG2E), mesh.shape["tp"], mesh.shape["cp"])
    blk = lambda a: pl.BlockSpec((1,) + a.shape[1:], lambda n, t: (n, 0, 0))
    hbm = pl.BlockSpec(memory_space=pltpu.HBM)
    dma = pltpu.SemaphoreType.DMA
    sds = jax.ShapeDtypeStruct
    ost = sds((G, 2, BL, VD), BF16)
    stat = pltpu.VMEM((H, R, LANES), F32)
    return pl.pallas_call(
        functools.partial(attn_kernel, dims),
        grid_spec=pltpu.PrefetchScalarGridSpec(
            num_scalar_prefetch=1, grid=(G,),
            in_specs=[blk(q_own), blk(q_par)] + [pl.BlockSpec((HALVES * BL, cs_own.shape[1]), lambda n, t: (n, 0))] * 2 + [hbm] * 4,
            out_specs=[hbm] * 4,
            scratch_shapes=[
                pltpu.VMEM((NB, BL, lat.shape[-1]), BF16), pltpu.VMEM((NB // 4, H, MXU, R), BF16), pltpu.VMEM((NB // 4, R, VD), BF16),
                pltpu.VMEM((H, 4, BL, MXU), BF16), pltpu.VMEM((H, R // HALVES, R), F32),
                pltpu.VMEM((H, NB // 4 - 1, R // HALVES, R), F32), pltpu.VMEM((H, 2, BL, R), F32), stat, stat, stat, pltpu.VMEM((HALVES, HALVES, BL, VD), BF16),
                pltpu.VMEM((KR, VD), BF16), pltpu.VMEM((VD, KR), BF16), pltpu.VMEM((KR, VD), BF16),
                dma((NB // HALVES,)), dma((HALVES,)), dma((HALVES,)), dma((G, 7)), dma((G, 7)), dma((3,)), dma((3,))],
        ),
        out_shape=[ost, ost, sds((4, 2, G, BL, VD), BF16), sds((mesh.shape["cp"],) + wf.shape, BF16)],
        compiler_params=pltpu.CompilerParams(collective_id=1, has_side_effects=True, vmem_limit_bytes=63 * MIB),
        cost_estimate=pl.CostEstimate(flops=G * H * T * R * 800, bytes_accessed=G * T * 640 * 2, transcendentals=0),
        name="attn",
    )(tab, q_own, q_par, cs_own, cs_par, w_uk, w_uv, lat, wf)


def proj_kernel(dims, pos, x, w_dq, w_dkv, w_uq, gq, gkv, fr, w_o,
                lat_all, latent, k_rope, q_own, q_par, wf, cs_own, cs_par, qn_o, qn_p,
                xbuf, wdq, wdkv, wuq, csb, pay, krb, kvb, qlat, qn, qst,
                xsem, wsem, dsem, csem, osem, wss, wrs, lss, lrs, qss, qrs, css, crs, lsem):
    n_tp, n_cp, n_t, half_cols, wc = dims
    me = Place(n_tp, n_cp)
    y, c, partner, right, left, far = me.y, me.c, me.partner, me.right, me.left, me.far

    rows = xbuf.shape[1]
    bl = pay.shape[3]
    kr_rank = gkv.shape[0]
    nj = WIDE
    last = n_t - 1
    every = HALVES * n_t

    def load_x(i):
        return pltpu.make_async_copy(x.at[pl.ds(pl.multiple_of(lax.rem(i, n_t) * rows, rows), rows), :], xbuf.at[lax.rem(i, HALVES)],
                                     xsem.at[lax.rem(i, HALVES)])

    kv_load = pltpu.make_async_copy(w_dkv, wdkv, wsem.at[0])
    kv_load.start()
    load_x(0).start()
    me.greet([(me.up, c), (me.dn, c), (me.dg, c), (y, partner), (y, right), (y, left)])
    half = lax.rem(y, HALVES)
    col_opp = pl.multiple_of((1 - half) * half_cols + c * wc, LANES)
    col_same = pl.multiple_of(half * half_cols + c * wc, LANES)
    w_sends = [me.copy(w_o.at[:, pl.ds(col, wc)], wf.at[k], wss.at[k], wrs.at[k], yy, c)
               for k, (col, yy) in enumerate(((col_opp, me.dn), (col_opp, me.up), (col_same, me.dg)))]
    for s in w_sends:
        s.start()

    def dq_load(j):
        cols = pl.ds(pl.multiple_of(j * nj, nj), nj)
        return pltpu.make_async_copy(w_dq.at[:, cols], wdq.at[:, cols], dsem.at[j])

    late = [pltpu.make_async_copy(w_uq.at[:, pl.ds(pl.multiple_of(me.core * wuq.shape[1], LANES), wuq.shape[1])], wuq, wsem.at[1])]

    def bid(n):
        return lax.div(pos[n, 0], bl)

    lane_b = lax.broadcasted_iota(jnp.int32, (bl, LANES), 1)
    row_b = lax.broadcasted_iota(jnp.int32, (bl, LANES), 0)
    sign = jnp.where(lax.rem(lane_b, HALF) < QUARTER, -1.0, 1.0)

    @pl.loop(0, every)
    def _(n):
        for k in range(HALVES):
            b = bid(n) if k == 0 else HALVES * n_cp - 1 - bid(n)
            ang = (b * bl + row_b).astype(F32) * fr[...]
            r = pl.ds(pl.multiple_of((HALVES * n + k) * bl, bl), bl)
            csb[r, :LANES] = jnp.cos(ang)
            csb[r, LANES:] = jnp.sin(ang) * sign

    cs_store = pltpu.make_async_copy(csb, cs_own, csem)
    cs_store.start()
    kv_load.wait()
    cs_store.wait()
    cs_send = me.copy(cs_own, cs_par, css, crs, y, partner)
    cs_send.start()

    lane = lax.broadcasted_iota(jnp.int32, (rows, LANES), 1)
    low32 = lax.rem(lane, HALF) < QUARTER
    upper = lax.broadcasted_iota(jnp.int32, (rows, LANES), 0) < rows // HALVES
    tile = lambda t: pl.ds(t * 2, HALVES)
    block = lambda t: pl.ds(pl.multiple_of(t * rows, rows), rows)

    def norm(t32, gain):
        return (t32 * lax.rsqrt(jnp.mean(t32 * t32, axis=-1, keepdims=True) + NORM_EPS) * gain).astype(BF16)

    def lat_copy(k, i, t, ref, yy, cc):
        return me.copy(ref, ref, lss.at[t, k], lrs.at[t, i], yy, cc)

    def own_store(t):
        return pltpu.make_async_copy(pay.at[lax.rem(t, HALVES)], lat_all.at[c, tile(t)], lsem.at[t])

    def out_stores(t):
        sl = lax.rem(t, HALVES)
        return [pltpu.make_async_copy(pay.at[sl, :, :, :, :kr_rank], latent.at[tile(t)], osem.at[0, sl]),
                pltpu.make_async_copy(krb.at[sl], k_rope.at[block(t)], osem.at[1, sl])]

    def send_own(t):
        own_store(t).wait()
        for k, cc in ((0, partner), (1, left), (2, right)):
            lat_copy(k, k, t, lat_all.at[c, tile(t)], y, cc).start()

    def settle_stores(t):
        for s in out_stores(t):
            s.wait()

    @pl.loop(0, n_t)
    def _(t):
        load_x(t).wait()

        pl.when(t == 0)(lambda: load_x(1).start())

        @pl.when(t == 1)
        def _():
            for j in range(wdq.shape[1] // nj):
                dq_load(j).start()
            for d in late:
                d.start()

        pl.when(t > 0)(lambda: send_own(t - 1))

        sl = lax.rem(t, HALVES)

        def kv_dot(wrows):
            d = lax.dot_general(xbuf[sl], wdkv[wrows, :], (((1,), (1,)), ((), ())), preferred_element_type=F32)
            return d.astype(BF16)

        @pl.loop(0, kr_rank // nj)
        def _(j):
            js = pl.ds(pl.multiple_of(j * nj, nj), nj)
            kvb[:, js] = kv_dot(js)

        u = kv_dot(pl.ds(kr_rank, wdkv.shape[0] - kr_rank)).astype(F32)
        pl.when(t + HALVES < n_t)(lambda: load_x(t + 2).start())
        lat = norm(kvb[...].astype(F32), gkv[...])
        u = jnp.concatenate([u, u], axis=1)
        w = jnp.where(low32, pltpu.roll(u, 96, 1), pltpu.roll(u, QUARTER, 1))
        rot = u * csb[block(t), :LANES] + w * csb[block(t), LANES:]
        pl.when(t >= HALVES)(lambda: settle_stores(t - 2))
        krb[sl] = rot[:, :HALF].astype(BF16)
        pay[sl, :, :, :, :kr_rank] = lat.reshape(HALVES, HALVES, bl, kr_rank)
        ids = jnp.where(upper, bid(HALVES * t), bid(HALVES * t + 1)).astype(F32)
        pay[sl, :, :, :, kr_rank:] = jnp.where(lane < HALF, rot, ids).astype(BF16).reshape(HALVES, HALVES, bl, LANES)
        for s in [own_store(t)] + out_stores(t):
            s.start()

    send_own(last)
    for d in late:
        d.wait()

    def stage1(t):
        rp, lp = lat_all.at[right, tile(t)], lat_all.at[left, tile(t)]
        lat_copy(3, 1, t, rp, y, partner).wait_recv()
        lat_copy(3, 2, t, lp, y, partner).wait_recv()
        for k, ref, cc in ((5, lat_all.at[left, tile(t), 0], right), (6, lat_all.at[right, tile(t), 1], left), (3, rp, partner), (4, lp, partner)):
            lat_copy(k, k, t, ref, y, cc).start()

    def stage2(t):
        for k in range(HALVES):
            ref = lat_all.at[far, tile(t), k]
            lat_copy(SPARE, 5 + k, t, ref, y, partner).wait_recv()
            lat_copy(7 + k, 7 + k, t, ref, y, partner).start()

    def project(src, wref, dst, width, before=None):
        @pl.loop(0, wref.shape[1] // width)
        def _(j):
            if before is not None:
                before(j)
            cols = pl.ds(pl.multiple_of(j * width, width), width)
            dst[:, cols] = jnp.dot(src[...], wref[:, cols], preferred_element_type=F32).astype(BF16)

    def q_store(u, dst, t):
        return pltpu.make_async_copy(qst.at[lax.rem(u, HALVES)], dst.at[block(t)], osem.at[3, lax.rem(u, HALVES)])

    def q_send(t):
        return me.copy(qn_o.at[block(t)], qn_p.at[block(t)], qss.at[t], qrs.at[t], y, partner)

    @pl.loop(0, n_t)
    def _(t):
        v = last - t
        pl.when(t >= HALVES)(lambda: load_x(v).wait())
        project(xbuf.at[lax.rem(v, HALVES)], wdq, qlat, nj, lambda j: pl.when(t == 0)(lambda: dq_load(j).wait()))
        pl.when(v >= HALVES)(lambda: load_x(v - 2).start())

        @pl.when(t == 0)
        def _():
            for k in (last - 1, last):
                settle_stores(k)

        stage1(t)
        sl = lax.rem(t, HALVES)
        qn[sl] = norm(qlat[...].astype(F32), gq[...])
        cp = pltpu.make_async_copy(qn.at[sl], qn_o.at[block(v)], osem.at[2, sl])
        cp.start()
        pl.when(t >= HALVES)(lambda: q_store(t, q_own, t - 2).wait())
        project(qn.at[sl], wuq, qst.at[sl], wuq.shape[1] // HALVES)
        cp.wait()
        q_send(v).start()
        q_store(t, q_own, v).start()

    def load_qp(t):
        return pltpu.make_async_copy(qn_p.at[block(last - t)], qn.at[lax.rem(t, HALVES)], osem.at[2, lax.rem(t, HALVES)])

    def take_qp(t):
        q_send(last - t).wait_recv()
        load_qp(t).start()

    take_qp(0)

    @pl.loop(0, n_t)
    def _(t):
        load_qp(t).wait()
        pl.when(t + 1 < n_t)(lambda: take_qp(t + 1))
        q_store(n_t + t, q_own, t).wait()
        project(qn.at[lax.rem(t, HALVES)], wuq, qst.at[lax.rem(n_t + t, HALVES)], wuq.shape[1] // HALVES)
        q_store(n_t + t, q_par, last - t).start()
        stage2(t)

    for k in range(HALVES):
        q_store(k, q_par, 0).wait()

    pr, pl_, pf = (lax.rem(partner + k, n_cp) for k in (HALVES, n_cp - 2, n_cp // HALVES))

    @pl.loop(0, n_t)
    def _(t):
        whole, part = lat_all.at[c, tile(t)], lat_all.at[c, tile(t), 0]
        for i, ref in ((0, lat_all.at[partner, tile(t)]), (3, lat_all.at[pr, tile(t)]), (4, lat_all.at[pl_, tile(t)]),
                       (7, lat_all.at[pf, tile(t), 0]), (8, lat_all.at[pf, tile(t), 1])):
            lat_copy(SPARE, i, t, ref, y, partner).wait_recv()
        for k in range(9):
            lat_copy(k, k, t, whole if k < 5 else part, y, partner).wait_send()
        q_send(t).wait_send()

    for s in w_sends + [cs_send]:
        s.wait()


def project_all(mesh, pos, x, w_dq, w_dkv, w_uq, g_q, g_kv, freq, w_o, bl):
    n_tp, n_cp = mesh.shape["tp"], mesh.shape["cp"]
    n_seq, seq, width = x.shape
    rows = HALVES * seq
    n_t = n_seq // HALVES
    rank, kvw = w_dq.shape[1], w_dkv.shape[1]
    kr = g_kv.shape[0]
    qw = w_uq.shape[1] // HALVES
    half_cols = width // HALVES
    wc = half_cols // n_cp
    total = n_seq * seq
    hbm = pl.BlockSpec(memory_space=pltpu.HBM)
    sds = jax.ShapeDtypeStruct
    dma = pltpu.SemaphoreType.DMA
    trig = sds((total, MXU), F32)
    return pl.pallas_call(
        functools.partial(proj_kernel, (n_tp, n_cp, n_t, half_cols, wc)),
        in_specs=[pl.BlockSpec(memory_space=pltpu.SMEM)] + [hbm] * 4 + [pl.BlockSpec(memory_space=pltpu.VMEM)] * 3 + [hbm],
        out_specs=[hbm] * 10,
        out_shape=[sds((n_cp, n_seq, 2, bl, kr + LANES), BF16), sds((n_seq, 2, bl, kr), BF16), sds((total, kvw - kr), BF16),
                   sds((total, qw), BF16), sds((total, qw), BF16), sds((3, w_o.shape[0], wc), BF16),
                   trig, trig, sds((total, rank), BF16), sds((total, rank), BF16)],
        scratch_shapes=[
            pltpu.VMEM((HALVES, rows, width), BF16), pltpu.VMEM((width, rank), BF16), pltpu.VMEM((kvw, width), BF16),
            pltpu.VMEM((rank, qw), BF16), pltpu.VMEM(trig.shape, F32), pltpu.VMEM((HALVES, HALVES, 2, bl, kr + LANES), BF16),
            pltpu.VMEM((HALVES, rows, kvw - kr), BF16), pltpu.VMEM((rows, kr), BF16), pltpu.VMEM((rows, rank), BF16),
            pltpu.VMEM((HALVES, rows, rank), BF16), pltpu.VMEM((HALVES, rows, qw), BF16),
            dma((HALVES,)), dma((HALVES,)), dma((rank // WIDE,)), dma, dma((4, HALVES)), dma((3,)), dma((3,)), dma((n_t, 9)), dma((n_t, 9)),
            dma((n_t,)), dma((n_t,)), dma, dma, dma((n_t,))],
        compiler_params=pltpu.CompilerParams(collective_id=0, has_side_effects=True, vmem_limit_bytes=63 * MIB),
        cost_estimate=pl.CostEstimate(flops=HALVES * total * (width * (rank + kvw) + HALVES * rank * qw), bytes_accessed=10**8,
                                      transcendentals=0),
        name="proj",
    )(pos, x.reshape(total, width), w_dq, w_dkv.T, w_uq, g_q, g_kv, freq, w_o)


def out_kernel(dims, x, w_o, wf, wx, ost_own, ost_par, obuf, out, wy, oy,
               wbuf, ov, xb, stage, wsem, osem, xsem, ssem, oss, ors, wss, wrs, ass, ars):
    n_tp, n_cp, n_seq, bl, half_cols = dims
    me = Place(n_tp, n_cp)
    cols, kb = xb.shape[-1], obuf.shape[-1]
    w, krows = cols // HALVES, w_o.shape[0]
    hk = krows // HALVES
    last = n_seq - 1
    half_of = lambda row: lax.rem(row, HALVES)
    tb = me.block(me.y, me.core)

    to_last = lambda s, p: oy.at[s, p, 1]
    to_prev = lambda s, p: oy.at[s, p, 0]
    prev_fwd = me.o_forwards(lambda s, p: obuf.at[s, p, last - 1], to_prev, oss.at[0], ors.at[0])
    last_sends = me.o_sends(ost_own.at[last], ost_par.at[last], to_last, oss.at[1], ors.at[1])
    last_fwd = me.o_forwards(to_last, to_last, oss.at[1], ors.at[1])
    def w_copy(k, src, dst, yy, cc):
        return me.copy(src, dst, wss.at[k], wrs.at[k], yy, cc)

    far_rows = pl.ds(0, hk), pl.ds(hk, hk)
    (to_r, to_l), (rest_r, rest_l) = w_parts(krows)
    p_right, p_left, p_far = (lax.rem(me.partner + k, n_cp) for k in (HALVES, n_cp - 2, n_cp // HALVES))
    mine, side = (me.y, me.partner), ((me.y, me.right), (me.y, me.left))

    def w_move(k, buf, dev, part, to):
        return w_copy(k, buf.at[dev, :, part], wy.at[dev, :, part], *to)

    w_sends = [w_copy(0, wf.at[:, rest_r], wy.at[me.c, :, rest_r], *side[0]), w_copy(1, wf.at[:, rest_l], wy.at[me.c, :, rest_l], *side[1]),
               w_move(2, wx, me.left, to_r, mine), w_move(3, wx, me.right, to_l, mine),
               w_move(4, wx, me.left, far_rows[0], side[0]), w_move(5, wx, me.right, far_rows[1], side[1])]
    rest_fwd = [w_move(6, wy, me.left, rest_r, mine), w_move(7, wy, me.right, rest_l, mine)]
    far_fwd = [w_move(8 + k, wy, me.far, far_rows[k], mine) for k in range(HALVES)]

    def w_recv(k, dev, part):
        w_move(k, wy, dev, part, mine).wait_recv()

    n_m = n_seq // HALVES
    rows = HALVES * bl
    k_of = (None, me.flip, 1 - me.flip, HALVES)
    every = pl.ds(0, krows)
    own = ((wx, to_l), (wy, rest_l)), ((wx, to_r), (wy, rest_r))
    pieces = ((((wf, every),), ((wx.at[me.partner], every),)),) + tuple(
        (tuple((buf.at[dev], part) for buf, part in own[i]), ((wy.at[dev_p], every),))
        for i, (dev, dev_p) in enumerate(((me.right, p_right), (me.left, p_left)))) + ((((wy.at[me.far], every),), ((wy.at[p_far], every),)),)
    offs = [pl.multiple_of(v * w, LANES) for v in (me.core, 1 - me.core)]

    def col_of(j, row):
        dx = j + (j // HALVES) * (1 - HALVES * (j % HALVES))
        xq = lax.rem(lax.div(me.c, HALVES) + dx, n_cp // HALVES)
        return pl.multiple_of(half_of(row) * half_cols + xq * cols, LANES)

    def w_loads(j):
        b = j % HALVES
        out_ = [pltpu.make_async_copy(w_o.at[:, pl.ds(col_of(j, me.y), cols)], wbuf.at[b, 0], wsem.at[b, 0])]
        for r in range(1, 4):
            for part in range(HALVES):
                for i, (buf, part_rows) in enumerate(pieces[j][part]):
                    out_.append(pltpu.make_async_copy(buf.at[k_of[r], part_rows], wbuf.at[b, r, part_rows, pl.ds(offs[part], w)],
                                                      wsem.at[b, HALVES * r + part + 8 * i]))
        return out_

    def x_load(j):
        return pltpu.make_async_copy(x.at[:, pl.ds(pl.multiple_of(tb * bl, bl), bl), pl.ds(col_of(j, me.y), cols)], xb.at[j % HALVES], xsem.at[j % HALVES])

    o_offs = [pl.multiple_of(v * kb, LANES) for v in (me.core, 1 - me.core)]

    def o_loads(n0, cnt, refs):
        out_ = []
        for i in range(cnt):
            for r in range(SOURCES):
                for part in range(HALVES):
                    src = ost_own.at[n0 + i, tb] if (r, part) == (0, 0) else refs(r, part, n0 + i)
                    out_.append(pltpu.make_async_copy(src, ov.at[n0 + i, :, pl.ds(pl.multiple_of(r * krows + o_offs[part], LANES), kb)],
                                                      osem.at[n0 + i, HALVES * r + part]))
        return out_

    early = o_loads(0, last - 1, lambda r, p, i: obuf.at[r, p, i])
    late = o_loads(last - 1, 2, lambda r, p, i: oy.at[r, p, i - last + 1] if (i == last or r == 3) else obuf.at[r, p, i])
    for d in w_loads(0) + early + [x_load(0)]:
        d.start()
    me.greet(((me.up, me.c), (me.dn, me.c), (me.up, me.partner), (me.dn, me.partner),
              (me.y, me.partner), (me.y, me.right), (me.y, me.left)))
    for s in last_sends + prev_fwd + w_sends:
        s.start()

    def region(row, j, m, n0=0, cnt=2):
        return out.at[pl.ds(HALVES * m + n0, cnt), pl.ds(pl.multiple_of(me.block(row, me.core) * bl, bl), bl), pl.ds(col_of(j, row), cols)]

    def ring(k, ref, j, m, yy):
        i = j * n_m + m
        return me.copy(ref, ref, ass.at[i, k], ars.at[i, k], yy, me.c)

    def tile_sends(j, m):
        ref = region(me.y, j, m)
        return ring(0, ref, j, m, me.up), ring(1, ref, j, m, me.dn)

    def forward(j, m):
        ring(0, region(me.dn, j, m), j, m, me.up).wait_recv()
        ring(2, region(me.dn, j, m, 0, 1), j, m, me.up).start()
        ring(1, region(me.up, j, m), j, m, me.up).wait_recv()
        ring(3, region(me.up, j, m, 1, 1), j, m, me.dn).start()

    nt = MXU

    def tile(j, m):
        b = j % HALVES

        @pl.loop(0, cols // nt)
        def _(t):
            cs_ = pl.ds(pl.multiple_of(t * nt, nt), nt)
            a = ov[pl.ds(HALVES * m, HALVES)].reshape(rows, 4 * krows)
            s = None
            for r in range(SOURCES):
                d = jnp.dot(a[:, r * krows:(r + 1) * krows], wbuf[b, r, :, cs_], preferred_element_type=F32)
                s = d if s is None else s + d
            xr = xb[b, pl.ds(HALVES * m, HALVES), :, cs_].reshape(rows, nt).astype(F32)
            stage[:, :, cs_] = (xr + s).astype(BF16).reshape(2, bl, nt)

        c = pltpu.make_async_copy(stage, region(me.y, j, m), ssem)
        c.start()
        c.wait()
        for s in tile_sends(j, m):
            s.start()

    def need(j):
        if j == 0:
            w_recv(1, me.right, rest_l)
            rest_fwd[1].start()
            w_recv(3, p_right, to_l)
            w_recv(7, p_right, rest_l)
        elif j == 1:
            w_recv(0, me.left, rest_r)
            rest_fwd[0].start()
            w_recv(2, p_left, to_r)
            w_recv(6, p_left, rest_r)
        else:
            for k in range(HALVES):
                w_recv(4 + k, me.far, far_rows[k])
                far_fwd[k].start()
            for k in range(HALVES):
                w_recv(8 + k, p_far, far_rows[k])
        for d in w_loads(j + 1) + [x_load(j + 1)]:
            d.start()

    def late_o():
        for k in (0, 2, 3):
            last_sends[k].wait_recv()
        for f in prev_fwd + last_fwd:
            f.wait_recv()
        for d in late:
            d.start()
        for d in late:
            d.wait()

    for k, f in zip((1, 4), last_fwd):
        last_sends[k].wait_recv()
        f.start()
    for d in early:
        d.wait()

    @pl.loop(0, 4 * n_m)
    def _(i):
        j, m = lax.div(i, n_m), lax.rem(i, n_m)
        for jj in range(SOURCES):
            @pl.when(i == jj * n_m)
            def _(jj=jj):
                for d in w_loads(jj) + [x_load(jj)]:
                    d.wait()
                if jj == 1:
                    need(jj)
        pl.when(i == n_m - 1)(late_o)
        tile(j, m)
        pl.when(i == 0)(lambda: need(0))

        @pl.when(j > 0)
        def _():
            forward(j - 1, m)

        pl.when(i == 3 * n_m - 1)(lambda: need(2))

    @pl.loop(0, n_m)
    def _(m):
        forward(3, m)

    @pl.loop(0, 4 * n_m)
    def _(i):
        j, m = lax.div(i, n_m), lax.rem(i, n_m)
        for k, row, n0, cnt in ((0, me.y, 0, HALVES), (1, me.y, 0, HALVES), (2, me.dn, 0, 1), (3, me.up, 1, 1)):
            r = region(row, j, m, n0, cnt)
            me.copy(r, r, ass.at[i, k], ars.at[i, k], me.up, me.c).wait_send()
        for k, n0 in ((HALVES, 0), (3, 1)):
            r = region(me.dg, j, m, n0, 1)
            me.copy(r, r, ass.at[i, k], ars.at[i, k], me.up, me.c).wait_recv()

    for s in last_sends + prev_fwd + last_fwd + w_sends + rest_fwd + far_fwd:
        s.wait_send()


def out_product(mesh, x, w_o, wf, wx, ost_own, ost_par, obuf):
    n_tp, n_cp = mesh.shape["tp"], mesh.shape["cp"]
    n_seq, seq, width = x.shape
    bl = seq // HALVES
    cols = HALVES * wf.shape[-1]
    krows = w_o.shape[0]
    hbm = pl.BlockSpec(memory_space=pltpu.HBM)
    dma = pltpu.SemaphoreType.DMA
    sds = jax.ShapeDtypeStruct
    tiles = HALVES * n_seq
    return pl.pallas_call(
        functools.partial(out_kernel, (n_tp, n_cp, n_seq, bl, width // HALVES)),
        in_specs=[hbm] * 7, out_specs=[hbm] * 3,
        out_shape=[sds(x.shape, BF16), sds(wx.shape, BF16), sds((4, 2, HALVES) + obuf.shape[3:], BF16)],
        scratch_shapes=[
            pltpu.VMEM((HALVES, 4, krows, cols), BF16), pltpu.VMEM((n_seq, bl, 4 * krows), BF16), pltpu.VMEM((HALVES, n_seq, bl, cols), BF16),
            pltpu.VMEM((HALVES, bl, cols), BF16), dma((HALVES, 16)), dma((n_seq, 8)), dma((HALVES,)), dma, dma((HALVES, 7)), dma((HALVES, 7)),
            dma((10,)), dma((10,)), dma((tiles, 4)), dma((tiles, 4))],
        compiler_params=pltpu.CompilerParams(collective_id=2, has_side_effects=True, vmem_limit_bytes=63 * MIB),
        cost_estimate=pl.CostEstimate(flops=n_seq * seq * cols * 16 * krows, bytes_accessed=10**8, transcendentals=0),
        name="outp",
    )(x, w_o, wf, wx, ost_own, ost_par, obuf)[0]


def settle_kernel(src, lat, kr, dst, lat_out, kr_out, buf, lbuf, kbuf, tbuf, rsem, wsem, lsem, ksem):
    n = buf.shape[0]
    reads = [pltpu.make_async_copy(src.at[i], buf.at[i], rsem.at[i]) for i in range(n)]
    writes = [pltpu.make_async_copy(buf.at[i], dst.at[i], wsem.at[i]) for i in range(n)]
    small = [pltpu.make_async_copy(*p) for p in ((kr, kbuf, ksem.at[0]), (lat, lbuf, lsem.at[0]))]
    small_out = [pltpu.make_async_copy(*p) for p in ((tbuf, kr_out, ksem.at[1]), (lbuf, lat_out, lsem.at[1]))]
    for d in small + reads:
        d.start()
    for d in small:
        d.wait()
    for i in range(tbuf.shape[0]):
        tbuf[i] = kbuf[i].astype(F32).T.astype(BF16)
    for d in small_out:
        d.start()
    for a, b in zip(reads, writes):
        a.wait()
        b.start()
    for d in writes + small_out:
        d.wait()


def settle(out, lat, kr):
    n_seq, seq, width = out.shape
    parts = 4 * n_seq
    shape = (parts, n_seq * seq // parts, width)
    lat_shape, kr_shape = (n_seq, seq, lat.shape[-1]), (n_seq, seq, kr.shape[-1])
    turned = (n_seq, kr.shape[-1], seq)
    hbm = pl.BlockSpec(memory_space=pltpu.HBM)
    sds = jax.ShapeDtypeStruct
    dma = pltpu.SemaphoreType.DMA
    a, b, c = pl.pallas_call(
        settle_kernel, in_specs=[hbm] * 3, out_specs=[hbm] * 3,
        out_shape=[sds(shape, BF16), sds(lat_shape, BF16), sds(turned, BF16)],
        scratch_shapes=[pltpu.VMEM(shape, BF16), pltpu.VMEM(lat_shape, BF16), pltpu.VMEM(kr_shape, BF16), pltpu.VMEM(turned, BF16),
                        dma((parts,)), dma((parts,)), dma((HALVES,)), dma((HALVES,))],
        compiler_params=pltpu.CompilerParams(vmem_limit_bytes=63 * MIB), name="settle",
    )(out.reshape(shape), lat.reshape(lat_shape), kr.reshape(kr_shape))
    return a.reshape(out.shape), b, jnp.swapaxes(c, 1, HALVES)


ROPE_BASE = 10000.0


def solution(mesh):
    def local_step(x, pos, w_dq, g_q, w_uq, w_dkv, g_kv, w_uk, w_uv, w_o):
        n_seq, seq, _ = x.shape
        n_cp = mesh.shape["cp"]
        bl = seq // HALVES
        nb = HALVES * n_cp
        kv_rank = g_kv.shape[0]
        rope = w_dkv.shape[1] - kv_rank
        heads = (w_uq.shape[1] - w_uk.shape[1]) // rope
        nope = w_uk.shape[1] // heads
        c = lax.axis_index("cp")
        core = c % HALVES

        freq = np.tile(ROPE_BASE ** (-2.0 * np.arange(rope // HALVES) / rope), LANES // (rope // HALVES))[None].astype(np.float32)
        lat_all, latent, k_rope, q_own, q_par, wf, cs_own, cs_par, _, _ = project_all(
            mesh, pos, x, w_dq, w_dkv, w_uq, g_q, g_kv, freq, w_o, bl)
        q_own, q_par = (a.reshape(n_seq, seq, -1) for a in (q_own, q_par))
        ids = lat_all[:, :, 0, 0, kv_rank + rope].astype(jnp.int32)
        blocks = jnp.arange(nb)
        first = ids[:, :, None] == blocks
        second = nb - 1 - ids[:, :, None] == blocks
        dev = jnp.arange(n_cp)[:, None, None]
        slots = jnp.sum(jnp.where(first, HALVES * dev, 0) + jnp.where(second, HALVES * dev + 1, 0), axis=0)
        mine = [jnp.sum(jnp.where(jnp.arange(n_cp)[:, None] == k, ids, 0), axis=0) for k in (c, c ^ 1)]
        last = nb // 4 - 1
        extra = []
        for i, b in enumerate(mine):
            is_first = b > last
            chunk = jnp.where(is_first, 1, last)
            extra += [jnp.where(is_first, i, 2 + i), chunk, jnp.where(is_first, b, nb - 1 - b) * bl - chunk * 4 * bl, is_first]
        tab = jnp.concatenate([slots, jnp.stack(mine + extra, axis=1).astype(jnp.int32)], axis=1).astype(jnp.int32)

        ost_own, ost_par, obuf, wx = attention(mesh, tab, q_own, q_par, cs_own, cs_par, w_uk, w_uv, lat_all, wf, (nope + rope) ** -0.5)
        return settle(out_product(mesh, x, w_o, wf, wx, ost_own, ost_par, obuf), latent, k_rope)

    seq_spec = P("dp", "cp", None)
    whole = P(None, None)
    in_specs = (seq_spec, P("dp", "cp"), whole, P(None), P(None, "tp"), whole, P(None), P(None, "tp"), P(None, "tp"), P("tp", None))
    return jax.shard_map(local_step, mesh=mesh, in_specs=in_specs, out_specs=(seq_spec,) * 3, check_vma=False)
```

time: 426 us -> 391 us (0.918)
  local copies, waits for them, and re-layouts: 14.1 us -> 1.02 us
  Pallas kernels: 398 us -> 387 us
  other arithmetic: 8.81 us -> 2.13 us
    unnamed x11 -> x0, local copies, waits for them, and re-layouts: 10.8 us -> none
    pallas_call x1, Pallas kernels: 189 us -> 180 us  [out_product(): pl.pallas_call(functools.partial(out_kernel, (n_tp, n_cp, n_seq, bl, widt...]
    pallas_call x1, Pallas kernels: 7.95 us -> 14.2 us  [settle(): pl.pallas_call(settle_kernel, in_specs=[hbm] * 3, out_specs=[hbm] * 3, ou...]
    pallas_call x1, Pallas kernels: 92 us -> 87.1 us  [project_all(): pl.pallas_call(functools.partial(proj_kernel, (n_tp, n_cp, n_t, half_cols...]
where the time goes in v2:
time: 391 us
  Pallas kernels  387 us (99%)
    pallas_call x1, Pallas kernels, out_product(): pl.pallas_call(functools.partial(out_kernel, (n_tp, n_cp, n_seq, bl, widt...  180 us
    pallas_call x1, Pallas kernels, attention(): pl.pallas_call(functools.partial(attn_kernel, dims), grid_spec=pltpu.Pref...  105 us
    pallas_call x1, Pallas kernels, project_all(): pl.pallas_call(functools.partial(proj_kernel, (n_tp, n_cp, n_t, half_cols...  87.1 us
    pallas_call x1, Pallas kernels, settle(): pl.pallas_call(settle_kernel, in_specs=[hbm] * 3, out_specs=[hbm] * 3, ou...  14.2 us

profile of v2, /device:TPU:97, one launch (start us, length us, event | category | flops | bytes accessed | tf_op | source)
XLA Modules:
  0.0 390.8 jit_solution(1032782229308065728)
XLA Ops:
  0.7 87.1 %proj.1 = (bf16[8,6,2,128,640]{4,3,2,1,0:T(8,128)(2,1)}, bf16[6,2,128,512]{3,2,1,0:T(8,128)(2,1)}, bf16[1536,64]{1,0:T(8,128)(2,1)}, bf16[1536,1536]{1,0:T(8,128...) custom-call(s32[6,256]{1,0:T(8,128)} %pos.1, ...), custom_call_target="tpu_custom_call" | custom-call | flops 54358179840 | bytes 100000000 | tf_op jit(solution)/shard_map/proj/pallas_call | solution.py:551
  87.8 1.9 convert_reduce_fusion
  89.7 0.1 copy.30
  89.8 0.1 select_reduce_fusion
  89.9 0.1 copy.38
  90.0 0.1 copy.39
  90.1 0.1 copy.31
  90.1 0.1 add_reduce_fusion
  90.3 0.7 concatenate.3.tab
  91.0 105.0 %attn.1 = (bf16[6,2,128,1024]{3,2,1,0:T(8,128)(2,1)}, bf16[6,2,128,1024]{3,2,1,0:T(8,128)(2,1)}, bf16[4,2,6,128,1024]{4,3,2,1,0:T(8,128)(2,1)}, bf16[8,3,2048,384]{3,2,1,0:T(8,128)(2,1)}) custom-call(s32[6,26]{1,0:T(8,128)} %concatenate.3.tab, bf16[6,256,1536]{2,1,0:T(8,128)(2,1)} %bitcast.20, bf16[6,256,1536]{2,1,0:T(8,128)(2,1)} %bitcast.21, ...), custom_call_target="tpu_custom_call" | custom-call | flops 40265318400 | bytes 15728640 | tf_op jit(solution)/shard_map/attn/pallas_call | solution.py:296
  196.0 180.4 %outp.1 = (bf16[6,256,6144]{2,1,0:T(8,128)(2,1)}, bf16[8,3,2048,384]{3,2,1,0:T(8,128)(2,1)}, bf16[4,2,2,128,1024]{4,3,2,1,0:T(8,128)(2,1)}) custom-call(bf16[6,256,6144]{2,1,0:T(8,128)(2,1)} %x.1, bf16[2048,6144]{1,0:T(8,128)(2,1)} %w_o.3, bf16[3,2048,384]{2,1,0:T(8,128)(2,1)} %get-tuple-element.19.refs_7_.wf, ...), custom_call_target="tpu_custom_call" | custom-call | flops 38654705664 | bytes 100000000 | tf_op jit(solution)/shard_map/outp/pallas_call | solution.py:780
  376.4 14.2 %settle.1 = (bf16[24,64,6144]{2,1,0:T(8,128)(2,1)}, bf16[6,256,512]{2,1,0:T(8,128)(2,1)}, bf16[6,64,256]{2,1,0:T(8,128)(2,1)}) custom-call(bf16[24,64,6144]{2,1,0:T(8,128)(2,1)} %bitcast.11, bf16[6,256,512]{2,1,0:T(8,128)(2,1)} %bitcast.12, bf16[6,256,64]{2,1,0:T(8,128)(2,1)} %bitcast.13), custom_call_target="tpu_custom_call" | custom-call | tf_op jit(solution)/shard_map/settle/pallas_call | solution.py:824
  (6 shorter events, 0.0 us)

commit v3 on v2

--- a/solution.py
+++ b/solution.py
@@ -65,11 +65,12 @@
 def attn_kernel(dims, tab, *refs):
     G, NB, BL, HP, scale2, n_tp, n_cp = dims
     CK = HALVES * BL
-    H = HALVES * HP
+    H, HG = HALVES * HP, HP
     q_own, q_par, cs_own, cs_par, w_uk, w_uv, lat, wf = refs[:8]
     ost_own, ost_par, obuf, wx = refs[8:12]
     latbuf, KT, V, Q, sF, sS, sX, mx, lsum, acc, ob, wk, wkT, wv, sem, ksem, osem, oss, ors, wss, wrs = refs[12:]
-    n = pl.program_id(0)
+    n, g = pl.program_id(0), pl.program_id(1)
+    u, U = HALVES * n + g, HALVES * G
     me = Place(n_tp, n_cp)
     rows_ = ((me.up, me.c), (me.dn, me.c), (me.up, me.partner), (me.dn, me.partner))
     w_to = ((me.y, me.partner), (me.y, me.right), (me.y, me.left))
@@ -83,21 +84,28 @@
     def copies(i):
         return [pltpu.make_async_copy(lat.at[p, i], latbuf.at[pl.ds(HALVES * p, HALVES)], sem.at[p]) for p in range(n_cp)]
 
+    def unit(ref, i):
+        w = ob.shape[-1]
+        return ref.at[lax.div(i, HALVES), :, :, pl.ds(pl.multiple_of(lax.rem(i, HALVES) * w, LANES), w)]
+
+    def landing(i):
+        w = ob.shape[-1]
+        return lambda s, p: obuf.at[s, p, lax.div(i, HALVES), :, pl.ds(pl.multiple_of(lax.rem(i, HALVES) * w, LANES), w)]
+
     def o_store(i):
-        return [pltpu.make_async_copy(ob.at[k], dst.at[i], osem.at[k]) for k, dst in enumerate((ost_own, ost_par))]
+        return [pltpu.make_async_copy(ob.at[k], unit(dst, i), osem.at[k]) for k, dst in enumerate((ost_own, ost_par))]
 
     def o_sends(i):
-        return me.o_sends(ost_own.at[i], ost_par.at[i], lambda s, p: obuf.at[s, p, i], oss.at[i], ors.at[i])
+        return me.o_sends(unit(ost_own, i), unit(ost_par, i), landing(i), oss.at[i], ors.at[i])
 
     def o_forwards(i):
-        at = lambda s, p: obuf.at[s, p, i]
-        return me.o_forwards(at, at, oss.at[i], ors.at[i])
+        return me.o_forwards(landing(i), landing(i), oss.at[i], ors.at[i])
 
     hw = wv.shape[1]
     kv_loads = [pltpu.make_async_copy(a.at[:, pl.ds(pl.multiple_of(me.core * hw, LANES), hw)], b, ksem.at[k])
                 for k, (a, b) in enumerate(((w_uk, wk), (w_uv, wv)))]
 
-    @pl.when(n == 0)
+    @pl.when(u == 0)
     def _():
         for c in copies(0) + kv_loads:
             c.start()
@@ -108,42 +116,45 @@
             c.wait()
         wkT[...] = wk[...].T
 
-    lane = lax.broadcasted_iota(jnp.int32, (BL, LANES), 1)
-    low64 = lane < HALF
-    low32 = lax.rem(lane, HALF) < QUARTER
-    for src_i, (q, cs) in enumerate(((q_own, cs_own), (q_par, cs_par))):
-        @pl.loop(0, HALVES)
-        def _(half, src_i=src_i, q=q, cs=cs):
-            r0 = half * 2 + src_i
-            rows = pl.ds(pl.multiple_of(half * BL, BL), BL)
-            ct = cs[rows, :LANES]
-            st = cs[rows, LANES:]
-            for p in range(HP):
-                a = q[0, rows, p * PAIR:p * PAIR + LANES]
-                b = q[0, rows, p * PAIR + LANES:p * PAIR + MXU].astype(F32)
-                c = q[0, rows, p * PAIR + MXU:p * PAIR + PAIR].astype(F32)
-                u = jnp.where(low64, b, c)
-                no = jnp.where(low64, c, b).astype(BF16)
-                w = jnp.where(low32, pltpu.roll(u, 96, 1), pltpu.roll(u, QUARTER, 1))
-                rot = (u * ct + w * st).astype(BF16)
-                Q[HALVES * p, r0, :, :LANES] = a
-                Q[HALVES * p, r0, :, LANES:MXU] = rot
-                Q[HALVES * p + 1, r0, :, :LANES] = no
-                Q[HALVES * p + 1, r0, :, LANES:MXU] = rot
-
-    @pl.when(n > 0)
+    @pl.when(g == 0)
     def _():
-        for c in o_store(n - 1):
+        lane = lax.broadcasted_iota(jnp.int32, (BL, LANES), 1)
+        low64 = lane < HALF
+        low32 = lax.rem(lane, HALF) < QUARTER
+        for src_i, (q, cs) in enumerate(((q_own, cs_own), (q_par, cs_par))):
+            @pl.loop(0, HALVES)
+            def _(half, src_i=src_i, q=q, cs=cs):
+                r0 = half * 2 + src_i
+                rows = pl.ds(pl.multiple_of(half * BL, BL), BL)
+                ct = cs[rows, :LANES]
+                st = cs[rows, LANES:]
+                for p in range(HP):
+                    a = q[0, rows, p * PAIR:p * PAIR + LANES]
+                    b = q[0, rows, p * PAIR + LANES:p * PAIR + MXU].astype(F32)
+                    c = q[0, rows, p * PAIR + MXU:p * PAIR + PAIR].astype(F32)
+                    u = jnp.where(low64, b, c)
+                    no = jnp.where(low64, c, b).astype(BF16)
+                    w = jnp.where(low32, pltpu.roll(u, 96, 1), pltpu.roll(u, QUARTER, 1))
+                    rot = (u * ct + w * st).astype(BF16)
+                    Q[HALVES * p, r0, :, :LANES] = a
+                    Q[HALVES * p, r0, :, LANES:MXU] = rot
+                    Q[HALVES * p + 1, r0, :, :LANES] = no
+                    Q[HALVES * p + 1, r0, :, LANES:MXU] = rot
+
+        for c in copies(n):
             c.wait()
-        for s in o_sends(n - 1):
+
+    @pl.when(u > 0)
+    def _():
+        for c in o_store(u - 1):
+            c.wait()
+        for s in o_sends(u - 1):
             s.start()
-
-    for c in copies(n):
-        c.wait()
 
     WB = 4 * BL
     lane_k = lax.broadcasted_iota(jnp.int32, (WB, LANES), 1)
     KR = wkT.shape[1]
+    heads = pl.ds(pl.multiple_of(g * HG * LANES, LANES), HG * LANES)
 
     b0, b1 = tab[n, NB], tab[n, NB + 1]
 
@@ -154,14 +165,14 @@
         kr = jnp.where(lane_k < HALF, blocks[:, KR:].astype(F32), 0.0)
         krT = kr.T.astype(BF16)
         krO = jnp.concatenate([krT[HALF:], krT[:HALF]], axis=0)
-        kt = lax.dot_general(wkT[...], lt, (((1,), (1,)), ((), ())), preferred_element_type=F32).astype(BF16)
-        V[kc] = jnp.dot(lt, wv[...], preferred_element_type=F32).astype(BF16)
-        for h in range(H):
+        kt = lax.dot_general(wkT[heads, :], lt, (((1,), (1,)), ((), ())), preferred_element_type=F32).astype(BF16)
+        V[kc] = jnp.dot(lt, wv[:, heads], preferred_element_type=F32).astype(BF16)
+        for h in range(HG):
             k = kt[h * LANES:h * LANES + LANES]
             KT[kc, h, :LANES] = k if h % HALVES == 0 else jnp.concatenate([k[HALF:], k[:HALF]], axis=0)
             KT[kc, h, LANES:] = krT if h % HALVES == 0 else krO
 
-    @pl.when(n + 1 < G)
+    @pl.when(jnp.logical_and(g == 1, n + 1 < G))
     def _():
         for c in copies(n + 1):
             c.start()
@@ -174,7 +185,7 @@
     col = lax.broadcasted_iota(jnp.int32, (HR, WK), 1)
     dF = jnp.where(row < BL, b0 * BL + row, (b1 - 1) * BL + row) - col
     dS = jnp.where(row < BL, (NB - 1 - b0) * BL + row, (NB - 2 - b1) * BL + row) - col
-    rF, rS = slice(0, HR), slice(HR, R)
+    rF, rS = slice(HR), slice(HR, R)
     extra = []
     for i in range(HALVES):
         at = [tab[n, NB + 2 + 4 * i + k] for k in range(SOURCES)]
@@ -187,8 +198,8 @@
         return t if w == LANES else fold(t)
 
     def p1(c):
-        for h in range(H):
-            q = Q[h, 2:].reshape(HR, MXU) if c else Q[h].reshape(R, MXU)
+        for h in range(HG):
+            q = Q[g * HG + h, 2:].reshape(HR, MXU) if c else Q[g * HG + h].reshape(R, MXU)
             s = jnp.dot(q, KT[c, h], preferred_element_type=F32) * scale2
             if c == 0:
                 f = jnp.where(dF >= 0, s[:HR], NEG)
@@ -201,9 +212,9 @@
             mx[h, rS] = jnp.maximum(mx[h, rS], fold(s)) if c else fold(s)
 
     def p1x():
-        for h in range(H):
+        for h in range(HG):
             for i, (block, chunk, d, is_first, r_f, r_s) in enumerate(extra):
-                s = jnp.dot(Q[h, block], KT[chunk, h], preferred_element_type=F32) * scale2
+                s = jnp.dot(Q[g * HG + h, block], KT[chunk, h], preferred_element_type=F32) * scale2
                 s = jnp.where(d >= 0, s, NEG)
                 sX[h, i] = s
                 m = fold(s)
@@ -220,17 +231,17 @@
         return ls, jnp.dot(jnp.concatenate(es, axis=1), V[chunk, :, h * LANES:h * LANES + LANES], preferred_element_type=F32)
 
     def p2(c):
-        for h in range(H):
+        for h in range(HG):
             def load(js):
                 t = sS[h, c, :, js] - mx[h, rS]
                 return t if c else jnp.concatenate([sF[h, :, js] - mx[h, rF], t], axis=0)
             ls, pv = weigh(load, c, h)
-            r = rS if c else slice(0, R)
+            r = rS if c else slice(R)
             lsum[h, r] = lsum[h, r] + ls if c else ls
             acc[h, r] = acc[h, r] + pv if c else pv
 
     def p2x():
-        for h in range(H):
+        for h in range(HG):
             for i, (_, chunk, _, is_first, r_f, r_s) in enumerate(extra):
                 m = jnp.where(is_first, mx[h, r_f], mx[h, r_s])
                 ls, pv = weigh(lambda js: sX[h, i, :, js] - m, chunk, h)
@@ -240,23 +251,25 @@
                     total = acc[h, r] + pick(pv)
                     ob[i, k, :, h * LANES:h * LANES + LANES] = (total * (1.0 / jnp.sum(l, axis=1, keepdims=True))).astype(BF16)
 
-    stages = [functools.partial(f, c) for f in (p1, p2) for c in range(nS)]
-    stages.insert(nS, p1x)
-    for k, stage in enumerate(stages + [p2x]):
-        pl.when(n + k >= 0)(stage)
-
-    @pl.when(jnp.logical_and(n > 0, n + 1 < G))
+    for c in range(nS):
+        p1(c)
+    p1x()
+
+    @pl.when(u > 1)
     def _():
-        for k, f in zip((1, 4), o_forwards(n - 1)):
-            o_sends(n - 1)[k].wait_recv()
+        for k, f in zip((1, 4), o_forwards(u - 2)):
+            o_sends(u - 2)[k].wait_recv()
             f.start()
 
-    for c in o_store(n):
+    for c in range(nS):
+        p2(c)
+    p2x()
+    for c in o_store(u):
         c.start()
 
-    @pl.when(n == G - 1)
+    @pl.when(u == U - 1)
     def _():
-        for c in o_store(n):
+        for c in o_store(u):
             c.wait()
 
         def drain_forward(i, _):
@@ -264,16 +277,16 @@
                 f.wait()
             return 0
 
-        @pl.loop(0, G - 1)
+        @pl.loop(0, U - 1)
         def _(i):
             for k, s in enumerate(o_sends(i)):
                 s.wait_send()
                 if k in (0, 2, 3):
                     s.wait_recv()
 
-        lax.fori_loop(0, G - 2, drain_forward, 0)
+        lax.fori_loop(0, U - 2, drain_forward, 0)
         for k in (1, 4):
-            o_sends(G - 2)[k].wait_recv()
+            o_sends(U - 2)[k].wait_recv()
         for k, slot in enumerate((me.partner, me.left, me.right)):
             w_send(k, me.c).wait_send()
             w_send(k, slot).wait_recv()
@@ -287,24 +300,25 @@
     H = VD // LANES
     R = 4 * BL
     dims = (G, NB, BL, H // HALVES, float(soft_scale * LOG2E), mesh.shape["tp"], mesh.shape["cp"])
-    blk = lambda a: pl.BlockSpec((1,) + a.shape[1:], lambda n, t: (n, 0, 0))
+    blk = lambda a: pl.BlockSpec((1,) + a.shape[1:], lambda n, g, t: (n, 0, 0))
     hbm = pl.BlockSpec(memory_space=pltpu.HBM)
     dma = pltpu.SemaphoreType.DMA
     sds = jax.ShapeDtypeStruct
     ost = sds((G, 2, BL, VD), BF16)
-    stat = pltpu.VMEM((H, R, LANES), F32)
+    HG = H // HALVES
+    stat = pltpu.VMEM((HG, R, LANES), F32)
     return pl.pallas_call(
         functools.partial(attn_kernel, dims),
         grid_spec=pltpu.PrefetchScalarGridSpec(
-            num_scalar_prefetch=1, grid=(G,),
-            in_specs=[blk(q_own), blk(q_par)] + [pl.BlockSpec((HALVES * BL, cs_own.shape[1]), lambda n, t: (n, 0))] * 2 + [hbm] * 4,
+            num_scalar_prefetch=1, grid=(G, HALVES),
+            in_specs=[blk(q_own), blk(q_par)] + [pl.BlockSpec((HALVES * BL, cs_own.shape[1]), lambda n, g, t: (n, 0))] * 2 + [hbm] * 4,
             out_specs=[hbm] * 4,
             scratch_shapes=[
-                pltpu.VMEM((NB, BL, lat.shape[-1]), BF16), pltpu.VMEM((NB // 4, H, MXU, R), BF16), pltpu.VMEM((NB // 4, R, VD), BF16),
-                pltpu.VMEM((H, 4, BL, MXU), BF16), pltpu.VMEM((H, R // HALVES, R), F32),
-                pltpu.VMEM((H, NB // 4 - 1, R // HALVES, R), F32), pltpu.VMEM((H, 2, BL, R), F32), stat, stat, stat, pltpu.VMEM((HALVES, HALVES, BL, VD), BF16),
+                pltpu.VMEM((NB, BL, lat.shape[-1]), BF16), pltpu.VMEM((NB // 4, HG, MXU, R), BF16), pltpu.VMEM((NB // 4, R, VD // HALVES), BF16),
+                pltpu.VMEM((H, 4, BL, MXU), BF16), pltpu.VMEM((HG, R // HALVES, R), F32),
+                pltpu.VMEM((HG, NB // 4 - 1, R // HALVES, R), F32), pltpu.VMEM((HG, 2, BL, R), F32), stat, stat, stat, pltpu.VMEM((HALVES, HALVES, BL, VD // HALVES), BF16),
                 pltpu.VMEM((KR, VD), BF16), pltpu.VMEM((VD, KR), BF16), pltpu.VMEM((KR, VD), BF16),
-                dma((NB // HALVES,)), dma((HALVES,)), dma((HALVES,)), dma((G, 7)), dma((G, 7)), dma((3,)), dma((3,))],
+                dma((NB // HALVES,)), dma((HALVES,)), dma((HALVES,)), dma((HALVES * G, 7)), dma((HALVES * G, 7)), dma((3,)), dma((3,))],
         ),
         out_shape=[ost, ost, sds((4, 2, G, BL, VD), BF16), sds((mesh.shape["cp"],) + wf.shape, BF16)],
         compiler_params=pltpu.CompilerParams(collective_id=1, has_side_effects=True, vmem_limit_bytes=63 * MIB),
@@ -580,15 +594,17 @@
     half_of = lambda row: lax.rem(row, HALVES)
     tb = me.block(me.y, me.core)
 
+    hb = kb // HALVES
+    cut = [pl.ds(k * hb, hb) for k in range(HALVES)]
     to_last = lambda s, p: oy.at[s, p, 1]
     to_prev = lambda s, p: oy.at[s, p, 0]
-    prev_fwd = me.o_forwards(lambda s, p: obuf.at[s, p, last - 1], to_prev, oss.at[0], ors.at[0])
-    last_sends = me.o_sends(ost_own.at[last], ost_par.at[last], to_last, oss.at[1], ors.at[1])
+    prev_fwd = me.o_forwards(lambda s, p: obuf.at[s, p, last, :, cut[0]], to_prev, oss.at[0], ors.at[0])
+    last_sends = me.o_sends(ost_own.at[last, :, :, cut[1]], ost_par.at[last, :, :, cut[1]], to_last, oss.at[1], ors.at[1])
     last_fwd = me.o_forwards(to_last, to_last, oss.at[1], ors.at[1])
     def w_copy(k, src, dst, yy, cc):
         return me.copy(src, dst, wss.at[k], wrs.at[k], yy, cc)
 
-    far_rows = pl.ds(0, hk), pl.ds(hk, hk)
+    far_rows = [pl.ds(k * hk, hk) for k in range(HALVES)]
     (to_r, to_l), (rest_r, rest_l) = w_parts(krows)
     p_right, p_left, p_far = (lax.rem(me.partner + k, n_cp) for k in (HALVES, n_cp - 2, n_cp // HALVES))
     mine, side = (me.y, me.partner), ((me.y, me.right), (me.y, me.left))
@@ -635,18 +651,24 @@
 
     o_offs = [pl.multiple_of(v * kb, LANES) for v in (me.core, 1 - me.core)]
 
-    def o_loads(n0, cnt, refs):
-        out_ = []
-        for i in range(cnt):
-            for r in range(SOURCES):
-                for part in range(HALVES):
-                    src = ost_own.at[n0 + i, tb] if (r, part) == (0, 0) else refs(r, part, n0 + i)
-                    out_.append(pltpu.make_async_copy(src, ov.at[n0 + i, :, pl.ds(pl.multiple_of(r * krows + o_offs[part], LANES), kb)],
-                                                      osem.at[n0 + i, HALVES * r + part]))
-        return out_
-
-    early = o_loads(0, last - 1, lambda r, p, i: obuf.at[r, p, i])
-    late = o_loads(last - 1, 2, lambda r, p, i: oy.at[r, p, i - last + 1] if (i == last or r == 3) else obuf.at[r, p, i])
+    def o_place(i, r, part, half=None):
+        off = r * krows + o_offs[part] + (0 if half is None else half * hb)
+        return ov.at[i, :, pl.ds(pl.multiple_of(off, LANES), kb if half is None else hb)]
+
+    def o_load(i, r, part):
+        src = ost_own.at[i, tb] if (r, part) == (0, 0) else obuf.at[r, part, i]
+        return pltpu.make_async_copy(src, o_place(i, r, part), osem.at[i, HALVES * r + part])
+
+    pairs = [(r, part) for r in range(SOURCES) for part in range(HALVES)]
+    early = [o_load(i, r, part) for i in range(last - 1) for r, part in pairs]
+    late = [o_load(last - 1, r, part) for r, part in pairs]
+    for r, part in pairs:
+        for half in range(HALVES):
+            if (r, part) == (0, 0):
+                src = ost_own.at[last, tb, :, cut[half]]
+            else:
+                src = oy.at[r, part, half] if half == 1 or r == 3 else obuf.at[r, part, last, :, cut[0]]
+            late.append(pltpu.make_async_copy(src, o_place(last, r, part, half), osem.at[last, HALVES * r + part + 8 * half]))
     for d in w_loads(0) + early + [x_load(0)]:
         d.start()
     me.greet(((me.up, me.c), (me.dn, me.c), (me.up, me.partner), (me.dn, me.partner),
@@ -780,10 +802,10 @@
     return pl.pallas_call(
         functools.partial(out_kernel, (n_tp, n_cp, n_seq, bl, width // HALVES)),
         in_specs=[hbm] * 7, out_specs=[hbm] * 3,
-        out_shape=[sds(x.shape, BF16), sds(wx.shape, BF16), sds((4, 2, HALVES) + obuf.shape[3:], BF16)],
+        out_shape=[sds(x.shape, BF16), sds(wx.shape, BF16), sds((4, 2, 2, bl, obuf.shape[-1] // HALVES), BF16)],
         scratch_shapes=[
             pltpu.VMEM((HALVES, 4, krows, cols), BF16), pltpu.VMEM((n_seq, bl, 4 * krows), BF16), pltpu.VMEM((HALVES, n_seq, bl, cols), BF16),
-            pltpu.VMEM((HALVES, bl, cols), BF16), dma((HALVES, 16)), dma((n_seq, 8)), dma((HALVES,)), dma, dma((HALVES, 7)), dma((HALVES, 7)),
+            pltpu.VMEM((HALVES, bl, cols), BF16), dma((HALVES, 16)), dma((n_seq, 16)), dma((HALVES,)), dma, dma((HALVES, 7)), dma((HALVES, 7)),
             dma((10,)), dma((10,)), dma((tiles, 4)), dma((tiles, 4))],
         compiler_params=pltpu.CompilerParams(collective_id=2, has_side_effects=True, vmem_limit_bytes=63 * MIB),
         cost_estimate=pl.CostEstimate(flops=n_seq * seq * cols * 16 * krows, bytes_accessed=10**8, transcendentals=0),

time: 391 us -> 385 us (0.985)
  Pallas kernels: 387 us -> 381 us
    pallas_call x1, Pallas kernels: 180 us -> 170 us  [out_product(): pl.pallas_call(functools.partial(out_kernel, (n_tp, n_cp, n_seq, bl, widt...]
    pallas_call x1, Pallas kernels: 105 us -> 110 us  [attention(): pl.pallas_call(functools.partial(attn_kernel, dims), grid_spec=pltpu.Pref...]
where the time goes in v3:
time: 385 us
  Pallas kernels  381 us (99%)
    pallas_call x1, Pallas kernels, out_product(): pl.pallas_call(functools.partial(out_kernel, (n_tp, n_cp, n_seq, bl, widt...  170 us
    pallas_call x1, Pallas kernels, attention(): pl.pallas_call(functools.partial(attn_kernel, dims), grid_spec=pltpu.Pref...  110 us
    pallas_call x1, Pallas kernels, project_all(): pl.pallas_call(functools.partial(proj_kernel, (n_tp, n_cp, n_t, half_cols...  87.1 us
    pallas_call x1, Pallas kernels, settle(): pl.pallas_call(settle_kernel, in_specs=[hbm] * 3, out_specs=[hbm] * 3, ou...  14.2 us

profile of v3, /device:TPU:97, one launch (start us, length us, event | category | flops | bytes accessed | tf_op | source)
XLA Modules:
  0.0 385.0 jit_solution(2564894946325481274)
XLA Ops:
  0.7 87.1 %proj.1 = (bf16[8,6,2,128,640]{4,3,2,1,0:T(8,128)(2,1)}, bf16[6,2,128,512]{3,2,1,0:T(8,128)(2,1)}, bf16[1536,64]{1,0:T(8,128)(2,1)}, bf16[1536,1536]{1,0:T(8,128...) custom-call(s32[6,256]{1,0:T(8,128)} %pos.1, ...), custom_call_target="tpu_custom_call" | custom-call | flops 54358179840 | bytes 100000000 | tf_op jit(solution)/shard_map/proj/pallas_call | solution.py:565
  87.8 1.9 convert_reduce_fusion
  89.7 0.1 copy.30
  89.8 0.1 select_reduce_fusion
  89.8 0.1 copy.38
  89.9 0.1 copy.39
  90.0 0.1 copy.31
  90.1 0.1 add_reduce_fusion
  90.3 0.7 concatenate.3.tab
  90.9 109.5 %attn.1 = (bf16[6,2,128,1024]{3,2,1,0:T(8,128)(2,1)}, bf16[6,2,128,1024]{3,2,1,0:T(8,128)(2,1)}, bf16[4,2,6,128,1024]{4,3,2,1,0:T(8,128)(2,1)}, bf16[8,3,2048,384]{3,2,1,0:T(8,128)(2,1)}) custom-call(s32[6,26]{1,0:T(8,128)} %concatenate.3.tab, bf16[6,256,1536]{2,1,0:T(8,128)(2,1)} %bitcast.20, bf16[6,256,1536]{2,1,0:T(8,128)(2,1)} %bitcast.21, ...), custom_call_target="tpu_custom_call" | custom-call | flops 40265318400 | bytes 15728640 | tf_op jit(solution)/shard_map/attn/pallas_call | solution.py:310
  200.5 170.2 %outp.1 = (bf16[6,256,6144]{2,1,0:T(8,128)(2,1)}, bf16[8,3,2048,384]{3,2,1,0:T(8,128)(2,1)}, bf16[4,2,2,128,512]{4,3,2,1,0:T(8,128)(2,1)}) custom-call(bf16[6,256,6144]{2,1,0:T(8,128)(2,1)} %x.1, bf16[2048,6144]{1,0:T(8,128)(2,1)} %w_o.3, bf16[3,2048,384]{2,1,0:T(8,128)(2,1)} %get-tuple-element.19.refs_7_.wf, ...), custom_call_target="tpu_custom_call" | custom-call | flops 38654705664 | bytes 100000000 | tf_op jit(solution)/shard_map/outp/pallas_call | solution.py:802
  370.6 14.2 %settle.1 = (bf16[24,64,6144]{2,1,0:T(8,128)(2,1)}, bf16[6,256,512]{2,1,0:T(8,128)(2,1)}, bf16[6,64,256]{2,1,0:T(8,128)(2,1)}) custom-call(bf16[24,64,6144]{2,1,0:T(8,128)(2,1)} %bitcast.11, bf16[6,256,512]{2,1,0:T(8,128)(2,1)} %bitcast.12, bf16[6,256,64]{2,1,0:T(8,128)(2,1)} %bitcast.13), custom_call_target="tpu_custom_call" | custom-call | tf_op jit(solution)/shard_map/settle/pallas_call | solution.py:846
  (6 shorter events, 0.0 us)

commit v4 on v3

--- a/solution.py
+++ b/solution.py
@@ -13,6 +13,7 @@
 HALVES = 2
 SOURCES = 4
 MIB = 2**20
+FORWARDED, DIRECT = (1, 4), (0, 2, 3)
 SPARE = 7
 
 
@@ -27,7 +28,7 @@
         self.n_tp = n_tp
         self.core = lax.rem(c, HALVES)
         self.partner = c + 1 - HALVES * self.core
-        self.right, self.left, self.far = (lax.rem(c + k, n_cp) for k in (HALVES, n_cp - 2, n_cp // HALVES))
+        self.right, self.left, self.far = (lax.rem(c + k, n_cp) for k in (HALVES, n_cp - HALVES, n_cp // HALVES))
         self.up, self.dn, self.dg = (lax.rem(y + k, n_tp) for k in (1, n_tp - 1, n_tp // HALVES))
         self.flip = lax.rem(y + self.core, HALVES)
         self.mate = lax.rem(y + 1 + HALVES * self.flip, n_tp)
@@ -67,8 +68,8 @@
     CK = HALVES * BL
     H, HG = HALVES * HP, HP
     q_own, q_par, cs_own, cs_par, w_uk, w_uv, lat, wf = refs[:8]
-    ost_own, ost_par, obuf, wx = refs[8:12]
-    latbuf, KT, V, Q, sF, sS, sX, mx, lsum, acc, ob, wk, wkT, wv, sem, ksem, osem, oss, ors, wss, wrs = refs[12:]
+    ost_own, ost_par, obuf, wx, lf = refs[8:13]
+    latbuf, KT, V, Q, sF, sS, sX, mx, lsum, acc, ob, wk, wkT, wv, sem, ksem, osem, oss, ors, wss, wrs, fss, frs = refs[13:]
     n, g = pl.program_id(0), pl.program_id(1)
     u, U = HALVES * n + g, HALVES * G
     me = Place(n_tp, n_cp)
@@ -81,8 +82,25 @@
     def w_send(k, slot):
         return me.copy(wf.at[:, w_rows[k]], wx.at[slot, :, w_rows[k]], wss.at[k], wrs.at[k], *w_to[k])
 
+    tail = G - 2
+    p_far = lax.rem(me.partner + n_cp // HALVES, n_cp)
+    far_from = [lat.at[me.left, pl.ds(tail, HALVES), 0], lat.at[me.right, pl.ds(tail, HALVES), 1]] + [lf.at[0, :, k] for k in range(HALVES)]
+    far_to = [lf.at[0, :, k] for k in range(HALVES)] + [lf.at[1, :, k] for k in range(HALVES)]
+    far = [me.copy(a, b, fss.at[k], frs.at[k], *(w_to[1:] + w_to[:1] * HALVES)[k]) for k, (a, b) in enumerate(zip(far_from, far_to))]
+
+    def copy_in(src, dev):
+        return pltpu.make_async_copy(src, latbuf.at[pl.ds(HALVES * dev, HALVES)], sem.at[dev])
+
+    def start_lat(i):
+        for k in range(n_cp):
+            dev = lax.rem(me.c + k, n_cp)
+            away = jnp.logical_and(i >= tail, jnp.logical_or(dev == me.far, dev == p_far))
+            which = jnp.where(dev == me.far, 0, 1)
+            pl.when(jnp.logical_not(away))(lambda: copy_in(lat.at[dev, i], dev).start())
+            pl.when(away)(lambda: copy_in(lf.at[which, lax.rem(i, HALVES)], dev).start())
+
     def copies(i):
-        return [pltpu.make_async_copy(lat.at[p, i], latbuf.at[pl.ds(HALVES * p, HALVES)], sem.at[p]) for p in range(n_cp)]
+        return [copy_in(lat.at[p, i], p) for p in range(n_cp)]
 
     def unit(ref, i):
         w = ob.shape[-1]
@@ -107,11 +125,12 @@
 
     @pl.when(u == 0)
     def _():
-        for c in copies(0) + kv_loads:
+        for c in kv_loads:
             c.start()
+        start_lat(n)
         me.greet(rows_ + w_to)
-        for k in range(3):
-            w_send(k, me.c).start()
+        for s in far[:2] + [w_send(k, me.c) for k in range(3)]:
+            s.start()
         for c in kv_loads:
             c.wait()
         wkT[...] = wk[...].T
@@ -172,10 +191,18 @@
             KT[kc, h, :LANES] = k if h % HALVES == 0 else jnp.concatenate([k[HALF:], k[:HALF]], axis=0)
             KT[kc, h, LANES:] = krT if h % HALVES == 0 else krO
 
-    @pl.when(jnp.logical_and(g == 1, n + 1 < G))
+    @pl.when(u == G - 2)
     def _():
-        for c in copies(n + 1):
-            c.start()
+        for k in range(HALVES):
+            far[k].wait_recv()
+            far[2 + k].start()
+
+    @pl.when(u == HALVES * tail - 1)
+    def _():
+        for f in far[2:]:
+            f.wait_recv()
+
+    pl.when(jnp.logical_and(g == 1, n + 1 < G))(lambda: start_lat(n + 1))
 
     HR = HALVES * BL
     R = HALVES * HR
@@ -257,7 +284,7 @@
 
     @pl.when(u > 1)
     def _():
-        for k, f in zip((1, 4), o_forwards(u - 2)):
+        for k, f in zip(FORWARDED, o_forwards(u - 2)):
             o_sends(u - 2)[k].wait_recv()
             f.start()
 
@@ -281,12 +308,14 @@
         def _(i):
             for k, s in enumerate(o_sends(i)):
                 s.wait_send()
-                if k in (0, 2, 3):
+                if k in DIRECT:
                     s.wait_recv()
 
         lax.fori_loop(0, U - 2, drain_forward, 0)
-        for k in (1, 4):
+        for k in FORWARDED:
             o_sends(U - 2)[k].wait_recv()
+        for f in far:
+            f.wait_send()
         for k, slot in enumerate((me.partner, me.left, me.right)):
             w_send(k, me.c).wait_send()
             w_send(k, slot).wait_recv()
@@ -312,15 +341,16 @@
         grid_spec=pltpu.PrefetchScalarGridSpec(
             num_scalar_prefetch=1, grid=(G, HALVES),
             in_specs=[blk(q_own), blk(q_par)] + [pl.BlockSpec((HALVES * BL, cs_own.shape[1]), lambda n, g, t: (n, 0))] * 2 + [hbm] * 4,
-            out_specs=[hbm] * 4,
+            out_specs=[hbm] * 5,
             scratch_shapes=[
                 pltpu.VMEM((NB, BL, lat.shape[-1]), BF16), pltpu.VMEM((NB // 4, HG, MXU, R), BF16), pltpu.VMEM((NB // 4, R, VD // HALVES), BF16),
                 pltpu.VMEM((H, 4, BL, MXU), BF16), pltpu.VMEM((HG, R // HALVES, R), F32),
                 pltpu.VMEM((HG, NB // 4 - 1, R // HALVES, R), F32), pltpu.VMEM((HG, 2, BL, R), F32), stat, stat, stat, pltpu.VMEM((HALVES, HALVES, BL, VD // HALVES), BF16),
                 pltpu.VMEM((KR, VD), BF16), pltpu.VMEM((VD, KR), BF16), pltpu.VMEM((KR, VD), BF16),
-                dma((NB // HALVES,)), dma((HALVES,)), dma((HALVES,)), dma((HALVES * G, 7)), dma((HALVES * G, 7)), dma((3,)), dma((3,))],
+                dma((NB // HALVES,)), dma((HALVES,)), dma((HALVES,)), dma((HALVES * G, 7)), dma((HALVES * G, 7)), dma((3,)), dma((3,)), dma((SOURCES,)), dma((SOURCES,))],
         ),
-        out_shape=[ost, ost, sds((4, 2, G, BL, VD), BF16), sds((mesh.shape["cp"],) + wf.shape, BF16)],
+        out_shape=[ost, ost, sds((SOURCES, HALVES, G, BL, VD), BF16), sds((mesh.shape["cp"],) + wf.shape, BF16),
+                   sds((HALVES, HALVES) + lat.shape[2:], BF16)],
         compiler_params=pltpu.CompilerParams(collective_id=1, has_side_effects=True, vmem_limit_bytes=63 * MIB),
         cost_estimate=pl.CostEstimate(flops=G * H * T * R * 800, bytes_accessed=G * T * 640 * 2, transcendentals=0),
         name="attn",
@@ -383,14 +413,11 @@
     cs_store = pltpu.make_async_copy(csb, cs_own, csem)
     cs_store.start()
     kv_load.wait()
-    cs_store.wait()
-    cs_send = me.copy(cs_own, cs_par, css, crs, y, partner)
-    cs_send.start()
 
     lane = lax.broadcasted_iota(jnp.int32, (rows, LANES), 1)
     low32 = lax.rem(lane, HALF) < QUARTER
     upper = lax.broadcasted_iota(jnp.int32, (rows, LANES), 0) < rows // HALVES
-    tile = lambda t: pl.ds(t * 2, HALVES)
+    tile = lambda t: pl.ds(t * HALVES, HALVES)
     block = lambda t: pl.ds(pl.multiple_of(t * rows, rows), rows)
 
     def norm(t32, gain):
@@ -457,6 +484,9 @@
             s.start()
 
     send_own(last)
+    cs_store.wait()
+    cs_send = me.copy(cs_own, cs_par, css, crs, y, partner)
+    cs_send.start()
     for d in late:
         d.wait()
 
@@ -464,8 +494,18 @@
         rp, lp = lat_all.at[right, tile(t)], lat_all.at[left, tile(t)]
         lat_copy(3, 1, t, rp, y, partner).wait_recv()
         lat_copy(3, 2, t, lp, y, partner).wait_recv()
-        for k, ref, cc in ((5, lat_all.at[left, tile(t), 0], right), (6, lat_all.at[right, tile(t), 1], left), (3, rp, partner), (4, lp, partner)):
-            lat_copy(k, k, t, ref, y, cc).start()
+        for k, ref in ((3, rp), (4, lp)):
+            lat_copy(k, k, t, ref, y, partner).start()
+
+        @pl.when(t < last)
+        def _():
+            for k, ref, cc in ((5, lat_all.at[left, tile(t), 0], right), (6, lat_all.at[right, tile(t), 1], left)):
+                lat_copy(k, k, t, ref, y, cc).start()
+
+        pl.when(t == last)(lambda: lat_copy(5, 5, t, id_rows(left), y, right).start())
+
+    def id_rows(dev):
+        return lat_all.at[dev, tile(last), 0, pl.ds(0, 16)]
 
     def stage2(t):
         for k in range(HALVES):
@@ -526,23 +566,34 @@
         q_store(n_t + t, q_own, t).wait()
         project(qn.at[lax.rem(t, HALVES)], wuq, qst.at[lax.rem(n_t + t, HALVES)], wuq.shape[1] // HALVES)
         q_store(n_t + t, q_par, last - t).start()
-        stage2(t)
-
+        pl.when(t < last)(lambda: stage2(t))
+
+    lat_copy(SPARE, 5, last, id_rows(far), y, partner).wait_recv()
+    lat_copy(SPARE, 7, last, id_rows(far), y, partner).start()
     for k in range(HALVES):
         q_store(k, q_par, 0).wait()
 
-    pr, pl_, pf = (lax.rem(partner + k, n_cp) for k in (HALVES, n_cp - 2, n_cp // HALVES))
+    pr, pl_, pf = (lax.rem(partner + k, n_cp) for k in (HALVES, n_cp - HALVES, n_cp // HALVES))
 
     @pl.loop(0, n_t)
     def _(t):
-        whole, part = lat_all.at[c, tile(t)], lat_all.at[c, tile(t), 0]
-        for i, ref in ((0, lat_all.at[partner, tile(t)]), (3, lat_all.at[pr, tile(t)]), (4, lat_all.at[pl_, tile(t)]),
-                       (7, lat_all.at[pf, tile(t), 0]), (8, lat_all.at[pf, tile(t), 1])):
+        for i, ref in ((0, lat_all.at[partner, tile(t)]), (3, lat_all.at[pr, tile(t)]), (4, lat_all.at[pl_, tile(t)])):
             lat_copy(SPARE, i, t, ref, y, partner).wait_recv()
-        for k in range(9):
-            lat_copy(k, k, t, whole if k < 5 else part, y, partner).wait_send()
+        for k in range(5):
+            lat_copy(k, k, t, lat_all.at[c, tile(t)], y, partner).wait_send()
+
+        @pl.when(t < last)
+        def _():
+            for k in range(HALVES):
+                lat_copy(SPARE, 7 + k, t, lat_all.at[pf, tile(t), k], y, partner).wait_recv()
+            for k in range(5, 9):
+                lat_copy(k, k, t, lat_all.at[c, tile(t), 0], y, partner).wait_send()
+
         q_send(t).wait_send()
 
+    lat_copy(SPARE, 7, last, id_rows(pf), y, partner).wait_recv()
+    for k in (5, 7):
+        lat_copy(k, k, last, id_rows(c), y, partner).wait_send()
     for s in w_sends + [cs_send]:
         s.wait()
 
@@ -606,7 +657,7 @@
 
     far_rows = [pl.ds(k * hk, hk) for k in range(HALVES)]
     (to_r, to_l), (rest_r, rest_l) = w_parts(krows)
-    p_right, p_left, p_far = (lax.rem(me.partner + k, n_cp) for k in (HALVES, n_cp - 2, n_cp // HALVES))
+    p_right, p_left, p_far = (lax.rem(me.partner + k, n_cp) for k in (HALVES, n_cp - HALVES, n_cp // HALVES))
     mine, side = (me.y, me.partner), ((me.y, me.right), (me.y, me.left))
 
     def w_move(k, buf, dev, part, to):
@@ -639,7 +690,7 @@
     def w_loads(j):
         b = j % HALVES
         out_ = [pltpu.make_async_copy(w_o.at[:, pl.ds(col_of(j, me.y), cols)], wbuf.at[b, 0], wsem.at[b, 0])]
-        for r in range(1, 4):
+        for r in range(1, SOURCES):
             for part in range(HALVES):
                 for i, (buf, part_rows) in enumerate(pieces[j][part]):
                     out_.append(pltpu.make_async_copy(buf.at[k_of[r], part_rows], wbuf.at[b, r, part_rows, pl.ds(offs[part], w)],
@@ -701,7 +752,7 @@
         @pl.loop(0, cols // nt)
         def _(t):
             cs_ = pl.ds(pl.multiple_of(t * nt, nt), nt)
-            a = ov[pl.ds(HALVES * m, HALVES)].reshape(rows, 4 * krows)
+            a = ov[pl.ds(HALVES * m, HALVES)].reshape(rows, SOURCES * krows)
             s = None
             for r in range(SOURCES):
                 d = jnp.dot(a[:, r * krows:(r + 1) * krows], wbuf[b, r, :, cs_], preferred_element_type=F32)
@@ -736,7 +787,7 @@
             d.start()
 
     def late_o():
-        for k in (0, 2, 3):
+        for k in DIRECT:
             last_sends[k].wait_recv()
         for f in prev_fwd + last_fwd:
             f.wait_recv()
@@ -745,13 +796,13 @@
         for d in late:
             d.wait()
 
-    for k, f in zip((1, 4), last_fwd):
+    for k, f in zip(FORWARDED, last_fwd):
         last_sends[k].wait_recv()
         f.start()
     for d in early:
         d.wait()
 
-    @pl.loop(0, 4 * n_m)
+    @pl.loop(0, SOURCES * n_m)
     def _(i):
         j, m = lax.div(i, n_m), lax.rem(i, n_m)
         for jj in range(SOURCES):
@@ -775,7 +826,7 @@
     def _(m):
         forward(3, m)
 
-    @pl.loop(0, 4 * n_m)
+    @pl.loop(0, SOURCES * n_m)
     def _(i):
         j, m = lax.div(i, n_m), lax.rem(i, n_m)
         for k, row, n0, cnt in ((0, me.y, 0, HALVES), (1, me.y, 0, HALVES), (2, me.dn, 0, 1), (3, me.up, 1, 1)):
@@ -802,9 +853,9 @@
     return pl.pallas_call(
         functools.partial(out_kernel, (n_tp, n_cp, n_seq, bl, width // HALVES)),
         in_specs=[hbm] * 7, out_specs=[hbm] * 3,
-        out_shape=[sds(x.shape, BF16), sds(wx.shape, BF16), sds((4, 2, 2, bl, obuf.shape[-1] // HALVES), BF16)],
+        out_shape=[sds(x.shape, BF16), sds(wx.shape, BF16), sds((SOURCES, HALVES, HALVES, bl, obuf.shape[-1] // HALVES), BF16)],
         scratch_shapes=[
-            pltpu.VMEM((HALVES, 4, krows, cols), BF16), pltpu.VMEM((n_seq, bl, 4 * krows), BF16), pltpu.VMEM((HALVES, n_seq, bl, cols), BF16),
+            pltpu.VMEM((HALVES, SOURCES, krows, cols), BF16), pltpu.VMEM((n_seq, bl, SOURCES * krows), BF16), pltpu.VMEM((HALVES, n_seq, bl, cols), BF16),
             pltpu.VMEM((HALVES, bl, cols), BF16), dma((HALVES, 16)), dma((n_seq, 16)), dma((HALVES,)), dma, dma((HALVES, 7)), dma((HALVES, 7)),
             dma((10,)), dma((10,)), dma((tiles, 4)), dma((tiles, 4))],
         compiler_params=pltpu.CompilerParams(collective_id=2, has_side_effects=True, vmem_limit_bytes=63 * MIB),
@@ -888,7 +939,7 @@
             extra += [jnp.where(is_first, i, 2 + i), chunk, jnp.where(is_first, b, nb - 1 - b) * bl - chunk * 4 * bl, is_first]
         tab = jnp.concatenate([slots, jnp.stack(mine + extra, axis=1).astype(jnp.int32)], axis=1).astype(jnp.int32)
 
-        ost_own, ost_par, obuf, wx = attention(mesh, tab, q_own, q_par, cs_own, cs_par, w_uk, w_uv, lat_all, wf, (nope + rope) ** -0.5)
+        ost_own, ost_par, obuf, wx, _ = attention(mesh, tab, q_own, q_par, cs_own, cs_par, w_uk, w_uv, lat_all, wf, (nope + rope) ** -0.5)
         return settle(out_product(mesh, x, w_o, wf, wx, ost_own, ost_par, obuf), latent, k_rope)
 
     seq_spec = P("dp", "cp", None)

time: 385 us -> 384 us (level)
  no operation moved by 1% of the time
where the time goes in v4:
time: 384 us; the launch traced here: 383 us
  Pallas kernels  379 us (99%)
    pallas_call x1, Pallas kernels, out_product(): pl.pallas_call(functools.partial(out_kernel, (n_tp, n_cp, n_seq, bl, widt...  170 us
    pallas_call x1, Pallas kernels, attention(): pl.pallas_call(functools.partial(attn_kernel, dims), grid_spec=pltpu.Pref...  111 us
    pallas_call x1, Pallas kernels, project_all(): pl.pallas_call(functools.partial(proj_kernel, (n_tp, n_cp, n_t, half_cols...  83.3 us
    pallas_call x1, Pallas kernels, settle(): pl.pallas_call(settle_kernel, in_specs=[hbm] * 3, out_specs=[hbm] * 3, ou...  14.2 us

profile of v4, /device:TPU:97, one launch (start us, length us, event | category | flops | bytes accessed | tf_op | source)
XLA Modules:
  0.0 383.3 jit_solution(3169541643539347792)
XLA Ops:
  0.7 83.3 %proj.1 = (bf16[8,6,2,128,640]{4,3,2,1,0:T(8,128)(2,1)}, bf16[6,2,128,512]{3,2,1,0:T(8,128)(2,1)}, bf16[1536,64]{1,0:T(8,128)(2,1)}, bf16[1536,1536]{1,0:T(8,128...) custom-call(s32[6,256]{1,0:T(8,128)} %pos.1, ...), custom_call_target="tpu_custom_call" | custom-call | flops 54358179840 | bytes 100000000 | tf_op jit(solution)/shard_map/proj/pallas_call | solution.py:616
  84.0 1.9 convert_reduce_fusion
  85.9 0.1 copy.30
  86.0 0.1 select_reduce_fusion
  86.1 0.1 copy.38
  86.2 0.1 copy.39
  86.3 0.1 copy.31
  86.4 0.1 add_reduce_fusion
  86.5 0.7 concatenate.3.tab
  87.2 111.4 %attn.1 = (bf16[6,2,128,1024]{3,2,1,0:T(8,128)(2,1)}, bf16[6,2,128,1024]{3,2,1,0:T(8,128)(2,1)}, bf16[4,2,6,128,1024]{4,3,2,1,0:T(8,128)(2,1)}, bf16[8,3,2048,38...) custom-call(s32[6,26]{1,0:T(8,128)} %concatenate.3.tab, bf16[6,256,1536]{2,1,0:T(8,128)(2,1)} %bitcast.20, ...), custom_call_target="tpu_custom_call" | custom-call | flops 40265318400 | bytes 15728640 | tf_op jit(solution)/shard_map/attn/pallas_call | solution.py:339
  198.6 170.3 %outp.1 = (bf16[6,256,6144]{2,1,0:T(8,128)(2,1)}, bf16[8,3,2048,384]{3,2,1,0:T(8,128)(2,1)}, bf16[4,2,2,128,512]{4,3,2,1,0:T(8,128)(2,1)}) custom-call(bf16[6,256,6144]{2,1,0:T(8,128)(2,1)} %x.1, bf16[2048,6144]{1,0:T(8,128)(2,1)} %w_o.3, bf16[3,2048,384]{2,1,0:T(8,128)(2,1)} %get-tuple-element.19.refs_7_.wf, ...), custom_call_target="tpu_custom_call" | custom-call | flops 38654705664 | bytes 100000000 | tf_op jit(solution)/shard_map/outp/pallas_call | solution.py:853
  368.9 14.2 %settle.1 = (bf16[24,64,6144]{2,1,0:T(8,128)(2,1)}, bf16[6,256,512]{2,1,0:T(8,128)(2,1)}, bf16[6,64,256]{2,1,0:T(8,128)(2,1)}) custom-call(bf16[24,64,6144]{2,1,0:T(8,128)(2,1)} %bitcast.11, bf16[6,256,512]{2,1,0:T(8,128)(2,1)} %bitcast.12, bf16[6,256,64]{2,1,0:T(8,128)(2,1)} %bitcast.13), custom_call_target="tpu_custom_call" | custom-call | tf_op jit(solution)/shard_map/settle/pallas_call | solution.py:897
  (6 shorter events, 0.0 us)

commit v5 on v4

--- a/solution.py
+++ b/solution.py
@@ -59,7 +59,7 @@
 
 
 def w_parts(rows):
-    cut = rows // 8
+    cut = rows // 16
     return (pl.ds(0, rows - cut), pl.ds(cut, rows - cut)), (pl.ds(rows - cut, cut), pl.ds(0, cut))
 
 

time: 384 us -> 384 us (level)
  no operation moved by 1% of the time
where the time goes in v5:
time: 384 us; the launch traced here: 383 us
  Pallas kernels  379 us (99%)
    pallas_call x1, Pallas kernels, out_product(): pl.pallas_call(functools.partial(out_kernel, (n_tp, n_cp, n_seq, bl, widt...  170 us
    pallas_call x1, Pallas kernels, attention(): pl.pallas_call(functools.partial(attn_kernel, dims), grid_spec=pltpu.Pref...  112 us
    pallas_call x1, Pallas kernels, project_all(): pl.pallas_call(functools.partial(proj_kernel, (n_tp, n_cp, n_t, half_cols...  83.3 us
    pallas_call x1, Pallas kernels, settle(): pl.pallas_call(settle_kernel, in_specs=[hbm] * 3, out_specs=[hbm] * 3, ou...  14.2 us

profile of v5, /device:TPU:97, one launch (start us, length us, event | category | flops | bytes accessed | tf_op | source)
XLA Modules:
  0.0 383.3 jit_solution(12079683117744145960)
XLA Ops:
  0.7 83.3 %proj.1 = (bf16[8,6,2,128,640]{4,3,2,1,0:T(8,128)(2,1)}, bf16[6,2,128,512]{3,2,1,0:T(8,128)(2,1)}, bf16[1536,64]{1,0:T(8,128)(2,1)}, bf16[1536,1536]{1,0:T(8,128...) custom-call(s32[6,256]{1,0:T(8,128)} %pos.1, ...), custom_call_target="tpu_custom_call" | custom-call | flops 54358179840 | bytes 100000000 | tf_op jit(solution)/shard_map/proj/pallas_call | solution.py:616
  84.0 1.9 convert_reduce_fusion
  85.9 0.1 copy.30
  86.0 0.1 select_reduce_fusion
  86.1 0.1 copy.38
  86.2 0.1 copy.39
  86.3 0.1 copy.31
  86.4 0.1 add_reduce_fusion
  86.5 0.7 concatenate.3.tab
  87.2 111.8 %attn.1 = (bf16[6,2,128,1024]{3,2,1,0:T(8,128)(2,1)}, bf16[6,2,128,1024]{3,2,1,0:T(8,128)(2,1)}, bf16[4,2,6,128,1024]{4,3,2,1,0:T(8,128)(2,1)}, bf16[8,3,2048,38...) custom-call(s32[6,26]{1,0:T(8,128)} %concatenate.3.tab, bf16[6,256,1536]{2,1,0:T(8,128)(2,1)} %bitcast.20, ...), custom_call_target="tpu_custom_call" | custom-call | flops 40265318400 | bytes 15728640 | tf_op jit(solution)/shard_map/attn/pallas_call | solution.py:339
  199.0 169.9 %outp.1 = (bf16[6,256,6144]{2,1,0:T(8,128)(2,1)}, bf16[8,3,2048,384]{3,2,1,0:T(8,128)(2,1)}, bf16[4,2,2,128,512]{4,3,2,1,0:T(8,128)(2,1)}) custom-call(bf16[6,256,6144]{2,1,0:T(8,128)(2,1)} %x.1, bf16[2048,6144]{1,0:T(8,128)(2,1)} %w_o.3, bf16[3,2048,384]{2,1,0:T(8,128)(2,1)} %get-tuple-element.19.refs_7_.wf, ...), custom_call_target="tpu_custom_call" | custom-call | flops 38654705664 | bytes 100000000 | tf_op jit(solution)/shard_map/outp/pallas_call | solution.py:853
  368.9 14.2 %settle.1 = (bf16[24,64,6144]{2,1,0:T(8,128)(2,1)}, bf16[6,256,512]{2,1,0:T(8,128)(2,1)}, bf16[6,64,256]{2,1,0:T(8,128)(2,1)}) custom-call(bf16[24,64,6144]{2,1,0:T(8,128)(2,1)} %bitcast.11, bf16[6,256,512]{2,1,0:T(8,128)(2,1)} %bitcast.12, bf16[6,256,64]{2,1,0:T(8,128)(2,1)} %bitcast.13), custom_call_target="tpu_custom_call" | custom-call | tf_op jit(solution)/shard_map/settle/pallas_call | solution.py:897
  (6 shorter events, 0.0 us)
